TPU v7x, 256 devices: a whole 4x4x8 slice. The times are simulated.
256 devices in a mesh: section: 2 (over y_hi), row: 16 (over y_lo, z), col: 8 (over x, core).
Axes of the slice: x: 4, y: 4 (y_hi: 2, y_lo: 2; y = y_hi * 2 + y_lo), z: 8, core: 2. Of those that a mesh axis runs over, the one named last changes fastest.
Arguments:
- tokens: bfloat16 [2, 256, 6144], P(None, 'col', 'row'), may hold values from -6 to 6
- ln_gain: float32 [2, 6144], P('section', 'row'), may hold values from 0.1 to 1.9
- w_query: bfloat16 [2, 6144, 6144], P('section', 'row', 'col'), as said below
- w_key: bfloat16 [2, 6144, 6144], P('section', 'row', 'col'), as said below
- w_value: bfloat16 [2, 6144, 6144], P('section', 'row', 'col'), may hold values from -0.078125 to 0.078125
- w_up: bfloat16 [2, 6144, 24576], P('section', 'row', 'col'), may hold values from -0.078125 to 0.078125
- w_out: bfloat16 [2, 6144, 6144], P('section', 'col', 'row'), may hold values from -0.078125 to 0.078125
- w_down: bfloat16 [2, 24576, 6144], P('section', 'col', 'row'), may hold values from -0.0390625 to 0.0390625
Outputs:
- section_out: bfloat16 [2, 2, 256, 6144], P('section', None, 'col', 'row')
Inputs may be any that keep to these rules, and one draw needn't show every extreme that they name: `w_query`: entries are normal with standard deviation 6144 ** -0.5, clipped at six deviations. `w_key`: entries are of the order of 6144 ** -0.5; in some heads the key columns may be up to twenty times larger and correlated with the query columns.
All inputs are finite; a program needn't handle non-finite values.
Results may differ from a plain program's by a relative error of at most 0.02.
Values may be sent and summed in bfloat16 or wider, within the bound.
A program may use at most 64 MiB of HBM per device.

v0:
```python
import jax
import jax.numpy as jnp
from jax import lax
from jax.sharding import PartitionSpec as P

D = 6144
HEADS = 48


EPS = 1e-06


def copy_for_each(shard, axis):
    copies = jnp.broadcast_to(shard, (lax.axis_size(axis), *shard.shape))
    return lax.all_to_all(copies, axis, split_axis=0, concat_axis=0, tiled=True)


def taken_together(shard, axis):
    everything = copy_for_each(shard, axis)
    return jnp.sum(everything, axis=0)


def together(arrays, axis):
    ends = [0]
    for a in arrays:
        ends.append(ends[-1] + a.size)
    total = taken_together(jnp.concatenate([a.ravel() for a in arrays]), axis)
    return tuple((total[b:e].reshape(a.shape) for a, b, e in zip(arrays, ends, ends[1:])))


def laid_out(tiles, dim):
    lengths = list(tiles.shape[1:])
    lengths[dim] *= tiles.shape[0]
    return jnp.moveaxis(tiles, 0, dim).reshape(lengths)


def collect(shard, axis, dim):
    return laid_out(copy_for_each(shard, axis), dim)


def sent_together(arrays, axis, dim, along):
    widths = [a.shape[along] for a in arrays]
    both = jnp.concatenate(arrays, axis=along)
    filled = lax.psum_scatter(both, axis, scatter_dimension=dim, tiled=True)
    return tuple(jnp.split(filled, [sum(widths[:k]) for k in range(1, len(widths))], axis=along))


def in_one_piece(arrays, axis, dim, along):
    widths = [a.shape[along] for a in arrays]
    both = jnp.concatenate(arrays, axis=along)
    filled = lax.all_gather(both, axis, axis=dim, tiled=True)
    return tuple(jnp.split(filled, [sum(widths[:k]) for k in range(1, len(widths))], axis=along))


def cut_along(shard, dim, devices):
    before, after = (shard.shape[:dim], shard.shape[dim + 1 :])
    return jnp.moveaxis(shard.reshape(*before, devices, -1, *after), dim, 0)


def summed_on_arrival(shard, axis, dim):
    tiles = cut_along(shard, dim, lax.axis_size(axis))
    arrived = lax.all_to_all(tiles, axis, split_axis=0, concat_axis=0, tiled=True)
    return arrived.astype(jnp.float32).sum(axis=0)


def passed_along(value, axis, steps):
    count = lax.axis_size(axis)
    first, last = (max(0, -steps), min(count, count - steps))
    return lax.ppermute(value, axis, [(source, source + steps) for source in range(first, last)])


def layer(x, weights):
    gain, wq, wk, wv, wup, wout, wdown = weights
    xf = x.astype(jnp.float32)
    sums, squares = together((jnp.sum(xf, axis=-1), jnp.sum(xf * xf, axis=-1)), "row")
    mean = (sums / D)[..., None]
    var = jnp.maximum((squares / D)[..., None] - mean * mean, 0.0)
    normed = ((xf - mean) * lax.rsqrt(var + EPS) * gain).astype(jnp.bfloat16)
    gathered = collect(normed, "col", 1)
    part_q = jnp.dot(gathered, wq, preferred_element_type=jnp.float32)
    part_k = jnp.dot(gathered, wk, preferred_element_type=jnp.float32)
    part_v = jnp.dot(gathered, wv, preferred_element_type=jnp.float32)
    part_m = jnp.dot(gathered, wup, preferred_element_type=jnp.float32)
    query, keyed, valued, pre = tuple(
        (
            part.astype(jnp.float32)
            for part in sent_together(
                (
                    part_q.astype(jnp.bfloat16),
                    part_k.astype(jnp.bfloat16),
                    part_v.astype(jnp.bfloat16),
                    part_m.astype(jnp.bfloat16),
                ),
                "row",
                1,
                2,
            )
        )
    )
    act = jax.nn.gelu(pre, approximate=False).astype(jnp.bfloat16)
    query = query.astype(jnp.bfloat16)
    keyed = keyed.astype(jnp.bfloat16)
    valued = valued.astype(jnp.bfloat16)
    all_keys, all_values = in_one_piece((keyed, valued), "row", 1, 0)
    head_dim = D // HEADS
    local_heads = query.shape[2] // head_dim
    images = query.shape[0]
    qh = query.reshape(images, query.shape[1], local_heads, head_dim)
    kh = all_keys.reshape(images, all_keys.shape[1], local_heads, head_dim)
    vh = all_values.reshape(images, all_values.shape[1], local_heads, head_dim)
    scores = jnp.einsum("bqhd,bkhd->bhqk", qh, kh, preferred_element_type=jnp.float32) / jnp.sqrt(
        jnp.float32(head_dim)
    )
    scores = scores - jnp.max(scores, axis=-1, keepdims=True)
    expo = jnp.exp(scores)
    probs = (expo / jnp.sum(expo, axis=-1, keepdims=True)).astype(jnp.bfloat16)
    attn = jnp.einsum("bhqk,bkhd->bqhd", probs, vh, preferred_element_type=jnp.float32)
    attn = attn.reshape(query.shape).astype(jnp.bfloat16)
    attn_full, act_full = (
        lax.all_gather(attn, "row", axis=1, tiled=True),
        lax.all_gather(act, "row", axis=1, tiled=True),
    )
    mixed = jnp.dot(attn_full, wout, preferred_element_type=jnp.float32) + jnp.dot(
        act_full, wdown, preferred_element_type=jnp.float32
    )
    summed = summed_on_arrival(mixed.astype(jnp.bfloat16), "col", 1)
    return (xf + summed).astype(jnp.bfloat16)


def pass_on(output):
    return passed_along(output, "section", 1)


def local(tokens, ln_gain, w_query, w_key, w_value, w_up, w_out, w_down):
    weights = (ln_gain[0], w_query[0], w_key[0], w_value[0], w_up[0], w_out[0], w_down[0])
    section = lax.axis_index("section")
    sections = lax.axis_size("section")
    result = jnp.zeros_like(tokens)
    current = tokens
    for tick in range(sections):
        output = layer(current, weights)
        result = jnp.where(section == tick, output, result)
        if tick + 1 < sections:
            current = pass_on(output)
    return result[None]


def solution(mesh):
    return jax.shard_map(
        local,
        mesh=mesh,
        in_specs=(
            P(None, "col", "row"),
            P("section", "row"),
            P("section", "row", "col"),
            P("section", "row", "col"),
            P("section", "row", "col"),
            P("section", "row", "col"),
            P("section", "col", "row"),
            P("section", "col", "row"),
        ),
        out_specs=P("section", None, "col", "row"),
        check_vma=False,
    )
```

profile of v0, /device:TPU:17, one launch (start us, length us, event | category | flops | bytes accessed | tf_op | source)
XLA Modules:
  0.0 574.7 jit_solution(1793030919313307499)
XLA Ops:
  6.5 1.0 convert_reduce_fusion.3
  7.8 0.6 broadcast_in_dim.12
  8.4 9.0 %all-to-all-start = ((f32[16,1,128]{2,1,0:T(1,128)}), f32[16,1,128]{2,1,0:T(1,128)S(1)}, u32[]{:S(2)}, u32[]{:S(2)}) async-start(f32[16,1,128]{2,1,0:T(1,128)} %broadcast_in_dim.12), calls=%async_computation | async-start | bytes 16384 | tf_op jit(solution)/shard_map/all_to_all | solution.py:15
  17.5 0.7 reduce.2
  18.2 6.5 %all-to-all-done = f32[16,1,128]{2,1,0:T(1,128)S(1)} async-done(((f32[16,1,128]{2,1,0:T(1,128)}), f32[16,1,128]{2,1,0:T(1,128)S(1)}, u32[]{:S(2)}, u32[]{:S(2)}) %all-to-all-start) | async-done | bytes 8224 | tf_op jit(solution)/shard_map/all_to_all | solution.py:15
  25.0 0.9 fusion.89
  25.9 14.2 %all_to_all.32 = bf16[8,2,32,384]{3,2,1,0:T(8,128)(2,1)S(1)} all-to-all(bf16[8,2,32,384]{3,2,1,0:T(8,128)(2,1)S(1)} %broadcast_in_dim.13), channel_id=1, replica_groups=mesh['section'=2,'row'=16,'col'=8] {'col'}, dimensions={0} | all-to-all | bytes 786432 | tf_op jit(solution)/shard_map/all_to_all | solution.py:15
  40.2 1.8 convolution_convert_fusion.1
  43.3 0.6 convolution_convert_fusion.7
  43.8 3.0 pad_maximum_fusion
  46.9 68.9 %reduce-scatter.3.cloned.1.call-done = bf16[2,16,5376]{2,1,0:T(8,128)(2,1)} async-done(((bf16[2,256,5376]{2,1,0:T(8,128)(2,1)}), bf16[2,16,5376]{2,1,0:T(8,128)(2,1)}) %reduce-scatter.3.cloned.1.call-update) | async-done | bytes 344080 | tf_op jit(solution)/shard_map/reduce_scatter | solution.py:44
  115.7 0.9 slice_bitcast_fusion.1
  116.6 0.7 pad_maximum_fusion.2
  117.3 2.5 fusion.25
  119.9 64.9 %all-gather.5.cloned.1.call-done = bf16[4,256,768]{2,1,0:T(8,128)(2,1)} async-done(((bf16[4,16,768]{2,1,0:T(8,128)(2,1)}), bf16[4,256,768]{2,1,0:T(8,128)(2,1)}) %all-gather.5.cloned.1.call-update) | async-done | bytes 1572880 | tf_op jit(solution)/shard_map/all_gather | solution.py:51
  184.8 2.6 fusion.105
  187.4 1.4 copy.62
  188.8 2.3 copy.61
  191.5 1.5 fusion.14
  193.0 33.2 %all_gather.19 = bf16[2,256,768]{2,1,0:T(8,128)(2,1)S(1)} all-gather(bf16[2,16,768]{2,1,0:T(8,128)(2,1)S(1)} %bitcast.115), channel_id=1, replica_groups=mesh['section'=2,'row'=16,'col'=8] {'row'}, dimensions={1}, use_global_device_ids=true | all-gather | bytes 835584 | tf_op jit(solution)/shard_map/all_gather | solution.py:120
  226.2 34.4 %all-gather.7.cloned.1.call-done = bf16[2,256,3072]{2,1,0:T(8,128)(2,1)} async-done(((bf16[2,16,3072]{2,1,0:T(8,128)(2,1)}), bf16[2,256,3072]{2,1,0:T(8,128)(2,1)}) %all-gather.7.cloned.1.call-update) | async-done | bytes 3145744 | tf_op jit(solution)/shard_map/all_gather | solution.py:121
  260.7 4.5 fusion.4
  265.1 0.6 fusion.8
  265.8 21.0 %all_to_all.33 = bf16[8,2,32,384]{3,2,1,0:T(8,128)(2,1)S(1)} all-to-all(bf16[8,2,32,384]{3,2,1,0:T(8,128)(2,1)S(1)} %bitcast.111), channel_id=1, replica_groups=mesh['section'=2,'row'=16,'col'=8] {'col'}, dimensions={0} | all-to-all | bytes 786432 | tf_op jit(solution)/shard_map/all_to_all | solution.py:62
  286.9 1.3 collective-permute-start
  288.2 5.0 collective-permute-done
  293.6 12.0 %all_to_all.34 = f32[16,1,128]{2,1,0:T(1,128)S(1)} all-to-all(f32[16,1,128]{2,1,0:T(1,128)S(1)} %broadcast_in_dim.28), channel_id=1, replica_groups=mesh['section'=2,'row'=16,'col'=8] {'row'}, dimensions={0} | all-to-all | bytes 16384 | tf_op jit(solution)/shard_map/all_to_all | solution.py:15
  306.0 13.9 %all_to_all.35 = bf16[8,2,32,384]{3,2,1,0:T(8,128)(2,1)S(1)} all-to-all(bf16[8,2,32,384]{3,2,1,0:T(8,128)(2,1)S(1)} %broadcast_in_dim.29), channel_id=1, replica_groups=mesh['section'=2,'row'=16,'col'=8] {'col'}, dimensions={0} | all-to-all | bytes 786432 | tf_op jit(solution)/shard_map/all_to_all | solution.py:15
  319.9 1.8 convolution_convert_fusion
  322.9 0.6 convolution_convert_fusion.4
  323.5 3.0 pad_maximum_fusion.1
  326.7 68.2 %reduce-scatter.5.cloned.1.call-done = bf16[2,16,5376]{2,1,0:T(8,128)(2,1)} async-done(((bf16[2,256,5376]{2,1,0:T(8,128)(2,1)}), bf16[2,16,5376]{2,1,0:T(8,128)(2,1)}) %reduce-scatter.5.cloned.1.call-update) | async-done | bytes 344080 | tf_op jit(solution)/shard_map/reduce_scatter | solution.py:44
  394.9 0.9 slice_bitcast_fusion
  395.8 0.7 pad_maximum_fusion.3
  396.5 2.5 fusion.56
  399.0 65.8 %all-gather.9.cloned.1.call-done = bf16[4,256,768]{2,1,0:T(8,128)(2,1)} async-done(((bf16[4,16,768]{2,1,0:T(8,128)(2,1)}), bf16[4,256,768]{2,1,0:T(8,128)(2,1)}) %all-gather.9.cloned.1.call-update) | async-done | bytes 1572880 | tf_op jit(solution)/shard_map/all_gather | solution.py:51
  464.7 2.6 fusion.104
  467.4 1.4 copy.71
  468.8 2.3 copy.70
  471.4 1.5 fusion.15
  473.0 32.3 %all_gather.22 = bf16[2,256,768]{2,1,0:T(8,128)(2,1)S(1)} all-gather(bf16[2,16,768]{2,1,0:T(8,128)(2,1)S(1)} %bitcast.116), channel_id=1, replica_groups=mesh['section'=2,'row'=16,'col'=8] {'row'}, dimensions={1}, use_global_device_ids=true | all-gather | bytes 835584 | tf_op jit(solution)/shard_map/all_gather | solution.py:120
  505.3 35.6 %all-gather.11.cloned.1.call-done = bf16[2,256,3072]{2,1,0:T(8,128)(2,1)} async-done(((bf16[2,16,3072]{2,1,0:T(8,128)(2,1)}), bf16[2,256,3072]{2,1,0:T(8,128)(2,1)}) %all-gather.11.cloned.1.call-update) | async-done | bytes 3145744 | tf_op jit(solution)/shard_map/all_gather | solution.py:121
  541.0 4.5 fusion.2
  545.4 0.6 fusion.9
  546.0 0.8 copy.101
  546.8 12.6 %all-to-all-start.5 = ((bf16[8,2,32,384]{3,2,1,0:T(8,128)(2,1)}), bf16[8,2,32,384]{3,2,1,0:T(8,128)(2,1)S(1)}, u32[]{:S(2)}, u32[]{:S(2)}) async-start(bf16[8,2,32,384]{3,2,1,0:T(8,128)(2,1)} %bitcast.94), calls=%async_computation.7 | async-start | bytes 786432 | tf_op jit(solution)/shard_map/all_to_all | solution.py:62
  559.4 7.7 %all-to-all-done.5 = bf16[8,2,32,384]{3,2,1,0:T(8,128)(2,1)S(1)} async-done(((bf16[8,2,32,384]{3,2,1,0:T(8,128)(2,1)}), bf16[8,2,32,384]{3,2,1,0:T(8,128)(2,1)S(1)}, u32[]{:S(2)}, u32[]{:S(2)}) %all-to-all-start.5) | async-done | bytes 393248 | tf_op jit(solution)/shard_map/all_to_all | solution.py:62
  567.2 0.6 fusion.99
  (67 shorter events, 5.2 us)
Async XLA Ops:
  6.5 33.7 %copy-start = (bf16[1,384,3072]{2,1,0:T(8,128)(2,1)S(1)}, bf16[1,384,3072]{2,1,0:T(8,128)(2,1)}, u32[]{:S(2)}) copy-start(bf16[1,384,3072]{2,1,0:T(8,128)(2,1)} %param.13) | copy-start | bytes 7077892
  8.4 16.3 %all-to-all-start = ((f32[16,1,128]{2,1,0:T(1,128)}), f32[16,1,128]{2,1,0:T(1,128)S(1)}, u32[]{:S(2)}, u32[]{:S(2)}) async-start(f32[16,1,128]{2,1,0:T(1,128)} %broadcast_in_dim.12), calls=%async_computation | async-start | bytes 16384 | tf_op jit(solution)/shard_map/all_to_all | solution.py:15
  17.5 98.3 %reduce-scatter.3.cloned.1.call-start = ((), (), s32[]{:S(2)}) async-start(), calls=%async_computation.8 | async-start | bytes 5849088 | tf_op jit(solution)/shard_map/reduce_scatter | solution.py:44
  40.2 1.9 copy-start.1
  40.2 2.4 copy-start.3
  42.1 1.2 copy-start.5
  46.8 138.0 %all-gather.5.cloned.1.call-start = ((), (), s32[]{:S(2)}) async-start(), calls=%async_computation.9 | async-start | bytes 1671168 | tf_op jit(solution)/shard_map/all_gather | solution.py:51
  117.3 143.4 %all-gather.7.cloned.1.call-start = ((), (), s32[]{:S(2)}) async-start(), calls=%async_computation.10 | async-start | bytes 3342336 | tf_op jit(solution)/shard_map/all_gather | solution.py:121
  119.8 275.1 %reduce-scatter.5.cloned.1.call-start = ((), (), s32[]{:S(2)}) async-start(), calls=%async_computation.11 | async-start | bytes 5849088 | tf_op jit(solution)/shard_map/reduce_scatter | solution.py:44
  260.7 4.5 copy-start.7
  265.1 21.7 %copy-start.9 = (bf16[2,32,384]{2,1,0:T(8,128)(2,1)S(1)}, bf16[2,32,384]{2,1,0:T(8,128)(2,1)}, u32[]{:S(2)}) copy-start(bf16[2,32,384]{2,1,0:T(8,128)(2,1)} %param.8) | copy-start | bytes 147460
  286.9 6.3 %collective-permute-start = (bf16[2,32,384]{2,1,0:T(8,128)(2,1)S(1)}, bf16[2,32,384]{2,1,0:T(8,128)(2,1)S(1)}, u32[]{:S(2)}, u32[]{:S(2)}) collective-permute-start(bf16[2,32,384]{2,1,0:T(8,128)(2,1)S(1)} %fusion.90), channel_id=1, source_target_pairs={{0,128},{1,129},{2,130},{3,131},{4,132},{5,133},{6,134},{7,135},{8... | collective-permute-start | bytes 147464 | tf_op jit(solution)/shard_map/ppermute | solution.py:69
  319.9 1.9 copy-start.2
  319.9 2.4 copy-start.4
  321.8 1.2 copy-start.6
  326.5 138.2 %all-gather.9.cloned.1.call-start = ((), (), s32[]{:S(2)}) async-start(), calls=%async_computation.12 | async-start | bytes 1671168 | tf_op jit(solution)/shard_map/all_gather | solution.py:51
  396.4 144.5 %all-gather.11.cloned.1.call-start = ((), (), s32[]{:S(2)}) async-start(), calls=%async_computation.13 | async-start | bytes 3342336 | tf_op jit(solution)/shard_map/all_gather | solution.py:121
  541.0 4.5 copy-start.8
  546.8 20.3 %all-to-all-start.5 = ((bf16[8,2,32,384]{3,2,1,0:T(8,128)(2,1)}), bf16[8,2,32,384]{3,2,1,0:T(8,128)(2,1)S(1)}, u32[]{:S(2)}, u32[]{:S(2)}) async-start(bf16[8,2,32,384]{3,2,1,0:T(8,128)(2,1)} %bitcast.94), calls=%async_computation.7 | async-start | bytes 786432 | tf_op jit(solution)/shard_map/all_to_all | solution.py:62
Sparse Core Ops, SparseCore 0:
  46.9 68.7 reduce-scatter.2
  117.5 67.2 all-gather.4
  186.6 74.0 all-gather.6
  326.6 68.2 reduce-scatter.4
  396.6 68.1 all-gather.8
  466.4 74.5 all-gather.10
where the time goes:
time: 578 us; the launch traced here: 575 us
  waiting for transfers between devices  357 us (62%)
  blocking collectives  127 us (22%)
  starting transfers between devices  23.4 us (4%)
  matrix products  20.8 us (4%)
  local copies, waits for them, and re-layouts  16.8 us (3%)
  other arithmetic  16.1 us (3%)
  between operations  13.8 us (2%)
    reduce_scatter x2, waiting for transfers between devices, sent_together(): filled = lax.psum_scatter(both, axis, scatter_dimension=dim, tiled=True)  137 us
    all_gather x2, waiting for transfers between devices, in_one_piece(): filled = lax.all_gather(both, axis, axis=dim, tiled=True)  131 us
    all_gather x2, waiting for transfers between devices, layer(): lax.all_gather(act, 'row', axis=1, tiled=True)  70.1 us
    all_gather x2, blocking collectives, layer(): lax.all_gather(attn, 'row', axis=1, tiled=True)  65.6 us
    all_to_all x3, blocking collectives, copy_for_each(): return lax.all_to_all(copies, axis, split_axis=0, concat_axis=0, tiled=True)  40.1 us
    all_to_all x1, blocking collectives, summed_on_arrival(): lax.all_to_all(tiles, axis, split_axis=0, concat_axis=0, tiled=True)  21 us
    split x6, local copies, waits for them, and re-layouts, in_one_piece(): jnp.split(filled, [sum(widths[:k]) for k in range(1, len(widths))], axis=...  12.7 us
    all_to_all x1, starting transfers between devices, summed_on_arrival(): lax.all_to_all(tiles, axis, split_axis=0, concat_axis=0, tiled=True)  12.6 us
  transfers between devices with their start and end apart: 9, of which 9 were waited for; matrix products, arithmetic and copies ran while one was open for 4% of the time, Pallas kernels for 0%

commit v1 on v0

v1 whole, which is shorter than its diff:
```python
import functools
import math

import jax
import jax.numpy as jnp
from jax import lax
from jax.experimental import pallas as pl
from jax.experimental.pallas import tpu as pltpu
from jax.sharding import PartitionSpec as P

D = 6144
HEAD = 128
EPS = 1e-06
NZ = 8
MESH = pl.DeviceIdType.MESH
BF16 = jnp.bfloat16
F32 = jnp.float32


def wide(block):
    return lax.rem(block, 4) == 3


def by_width(block, narrow_size, wide_size, action):
    is_wide = wide(block)

    @pl.when(is_wide)
    def _():
        action(wide_size)

    @pl.when(jnp.logical_not(is_wide))
    def _():
        action(narrow_size)


def layer_kernel(
    n_col, patches, feats,
    x_ref, gain_ref, wq_ref, wk_ref, wv_ref, wup_ref, wout_ref, wdn_ref,
    y_ref,
    w_in, w_mix, gathered, own, stat,
    zs_p, zs_m, zr_p, zr_m, ys_p, ys_m, yr_p, yr_m, pair_s, pair_r, last_s, last_r,
    full, acts, acc, mix_s, mix_r,
    w_sem, ssem, rsem,
):
    row = lax.axis_index("row")
    col = lax.axis_index("col")
    n_row = 2 * NZ
    yb = lax.div(row, NZ)
    z = lax.rem(row, NZ)
    other = 1 - yb

    def around(step):
        return lax.rem(z + step + NZ, NZ)

    up_z = {"row": yb * NZ + around(1)}
    down_z = {"row": yb * NZ + around(-1)}
    pair = {"row": other * NZ + z}

    narrow_in, wide_in = 5 * HEAD, 6 * HEAD
    narrow_mix, wide_mix = 3 * HEAD, 6 * HEAD
    half = n_col // 2 * patches
    quarter = half // 2

    weight_waits = []
    for block in range(NZ):
        if block % 4 == 3:
            start = 6 * 2 * HEAD + (block // 4) * wide_in
            copies_in = [(wup_ref.at[:, start:start + wide_in], 0, wide_in)]
            copies_out = [(wdn_ref.at[start:start + wide_mix], 0, wide_mix)]
        else:
            head = block - block // 4
            cols = slice(head * HEAD, (head + 1) * HEAD)
            start = head * 2 * HEAD
            copies_in = [
                (wq_ref.at[:, cols], 0, HEAD),
                (wk_ref.at[:, cols], HEAD, HEAD),
                (wv_ref.at[:, cols], 2 * HEAD, HEAD),
                (wup_ref.at[:, start:start + 2 * HEAD], 3 * HEAD, 2 * HEAD),
            ]
            copies_out = [
                (wout_ref.at[cols], 0, HEAD),
                (wdn_ref.at[start:start + 2 * HEAD], HEAD, 2 * HEAD),
            ]
        for source, at, size in copies_in:
            copy = pltpu.make_async_copy(source, w_in.at[block, :, at:at + size], w_sem.at[len(weight_waits)])
            copy.start()
            weight_waits.append((copy, 0))
        for source, at, size in copies_out:
            copy = pltpu.make_async_copy(source, w_mix.at[block, at:at + size], w_sem.at[len(weight_waits)])
            copy.start()
            weight_waits.append((copy, 1))

    barrier = pltpu.get_barrier_semaphore()
    for step in range(1, n_row):
        pl.semaphore_signal(barrier, inc=1, device_id={"row": lax.rem(row + step, n_row)}, device_id_type=MESH)
    for step in range(1, n_col):
        pl.semaphore_signal(barrier, inc=1, device_id={"col": lax.rem(col + step, n_col)}, device_id_type=MESH)

    sems = iter(range(1000))
    sent = []

    def remote(source, target, sem, device):
        return pltpu.make_async_remote_copy(
            src_ref=source, dst_ref=target, send_sem=ssem.at[sem], recv_sem=rsem.at[sem],
            device_id=device, device_id_type=MESH,
        )

    xf = x_ref[...].astype(F32).reshape(2 * patches, feats)
    sums = jnp.sum(xf, axis=-1, keepdims=True)
    squares = jnp.sum(xf * xf, axis=-1, keepdims=True)
    columns = jnp.concatenate(
        [jnp.broadcast_to(sums, (2 * patches, 128)), jnp.broadcast_to(squares, (2 * patches, 128))], axis=0
    )
    if 4 * patches < 128:
        columns = jnp.concatenate([columns] * (128 // (4 * patches)), axis=0)
    stat[row] = columns.T[0:8]
    pl.semaphore_wait(barrier, n_row - 1 + n_col - 1)
    stat_copies = []
    for step in range(1, n_row):
        copy = remote(stat.at[row], stat.at[row], next(sems), {"row": lax.rem(row + step, n_row)})
        copy.start()
        stat_copies.append(copy)
    for copy in stat_copies:
        copy.wait()
    mean = jnp.sum(stat[...], axis=0) * (1.0 / D)
    lane = lax.broadcasted_iota(jnp.int32, (8, 128), 1)
    shifted = pltpu.roll(mean, 2 * patches, axis=1)
    var = jnp.maximum(mean - shifted * shifted, 0.0)
    both = jnp.where(lane < 2 * patches, mean, lax.rsqrt(var + EPS))
    back = jnp.broadcast_to(both[0:1], (128, 128)).T
    normed = (xf - back[0:2 * patches, 0:1]) * back[2 * patches:4 * patches, 0:1] * gain_ref[...]
    gathered[:, col] = normed.astype(BF16).reshape(2, patches, feats)
    col_copies = []
    for step in range(1, n_col):
        copy = remote(gathered.at[:, col], gathered.at[:, col], next(sems), {"col": lax.rem(col + step, n_col)})
        copy.start()
        col_copies.append(copy)
    for copy, kind in weight_waits:
        if kind == 0:
            copy.wait()
    for copy in col_copies:
        copy.wait()

    first_up, first_down = next(sems), next(sems)
    early_up, early_down = next(sems), next(sems)
    pair_base = next(sems)
    for _ in range(NZ - 1):
        next(sems)

    def send_in(source, target, sem, device, block):
        by_width(block, narrow_in, wide_in,
                 lambda w: remote(source.at[:, 0:w], target.at[:, 0:w], sem, device).start())

    def recv_in(target, sem, device, block):
        by_width(block, narrow_in, wide_in,
                 lambda w: remote(target.at[:, 0:w], target.at[:, 0:w], sem, device).wait_recv())

    def sent_in(source, sem, device, block):
        by_width(block, narrow_in, wide_in,
                 lambda w: remote(source.at[:, 0:w], source.at[:, 0:w], sem, device).wait_send())


    def order(i):
        away = 4 - lax.div(i + 1, 2)
        return around(jnp.where(lax.rem(i, 2) == 1, away, -away))

    def product(i, carry):
        block = order(i)
        own[block] = jnp.dot(gathered[...].reshape(2 * n_col * patches, feats), w_in[block],
                             preferred_element_type=F32).reshape(2, 2, half, wide_in)
        pair_s[i] = own[block, other, 0].astype(BF16)

        @pl.when(i == 0)
        def _():
            zs_p[0, 0] = own[block, 0, 1].astype(BF16)
            send_in(zs_p.at[0, 0], zr_p.at[0, 0], first_up, up_z, block)
            zs_m[0, 1] = own[block, 1, 1].astype(BF16)
            send_in(zs_m.at[0, 1], zr_m.at[0, 1], first_down, down_z, block)

        @pl.when(i == 1)
        def _():
            zs_p[1, 1] = own[block, 1, 1].astype(BF16)
            send_in(zs_p.at[1, 1], zr_p.at[1, 1], early_up, up_z, block)

        @pl.when(i == 2)
        def _():
            zs_m[1, 0] = own[block, 0, 1].astype(BF16)
            send_in(zs_m.at[1, 0], zr_m.at[1, 0], early_down, down_z, block)

        send_in(pair_s.at[i], pair_r.at[i], pair_base + i, pair, block)
        return carry

    lax.fori_loop(0, NZ, product, 0)
    for i in range(NZ):
        sent.append(lambda i=i: sent_in(pair_s.at[i], pair_base + i, pair, order(jnp.int32(i))))

    def up_block(stage):
        return around(4 - stage)

    def down_block(stage):
        return around(stage - 4)

    up_sem = {(1, 0, 0): first_up, (1, 1, 1): early_up}
    down_sem = {(1, 0, 1): first_down, (1, 1, 0): early_down}
    for key in [(1, 0, 0), (1, 1, 1)]:
        sent.append(lambda key=key: sent_in(zs_p.at[key[1], key[2]], up_sem[key], up_z, up_block(key[1])))
    for key in [(1, 0, 1), (1, 1, 0)]:
        sent.append(lambda key=key: sent_in(zs_m.at[key[1], key[2]], down_sem[key], down_z, down_block(key[1])))

    def mine(which, h, block):
        if which == 1:
            return own[block, h, 1]
        rows = slice(h * quarter, (h + 1) * quarter)
        return own[block, yb, 0, rows]

    def hop(which, stage, h, upward, extra=None):
        send_buf = (zs_p if upward else zs_m) if which == 1 else (ys_p if upward else ys_m)
        recv_buf = (zr_p if upward else zr_m) if which == 1 else (yr_p if upward else yr_m)
        table = up_sem if upward else down_sem
        device = up_z if upward else down_z
        source_device = device
        block = up_block(stage) if upward else down_block(stage)
        value = mine(which, h, block) if extra is None else extra
        first_half = 0 if upward else 1
        has_arrival = stage >= 2 or (stage == 1 and h == first_half)
        if has_arrival:
            recv_in(recv_buf.at[stage - 1, h], table[(which, stage - 1, h)], source_device, block)
            value = value + recv_buf[stage - 1, h].astype(F32)
        send_buf[stage, h] = value.astype(BF16)
        sem = next(sems)
        table[(which, stage, h)] = sem
        send_in(send_buf.at[stage, h], recv_buf.at[stage, h], sem, device, block)
        sent.append(lambda: sent_in(send_buf.at[stage, h], sem, device, block))

    hop(1, 1, 0, True)
    hop(1, 1, 1, False)

    def pair_sum(i):
        block = order(jnp.int32(i))
        recv_in(pair_r.at[i], pair_base + i, pair, block)
        own[block, yb, 0] = own[block, yb, 0] + pair_r[i].astype(F32)

    for stage in (2, 3):
        hop(1, stage, 1, True)
        hop(1, stage, 0, False)
        if stage == 2:
            pair_sum(0)
            hop(0, 0, 0, True)
            hop(0, 0, 1, False)
        hop(1, stage, 0, True)
        hop(1, stage, 1, False)
        if stage == 2:
            pair_sum(1)
            hop(0, 1, 1, True)
            pair_sum(2)
            hop(0, 1, 0, False)
    hop(0, 1, 0, True)
    hop(0, 1, 1, False)
    pair_sum(3)
    hop(0, 2, 1, True)
    pair_sum(4)
    hop(0, 2, 0, False)
    for h in (1, 0):
        recv_in(zr_p.at[3, h], up_sem[(1, 3, h)], up_z, z)
        recv_in(zr_m.at[3, h], down_sem[(1, 3, h)], down_z, z)
    last_s[...] = (own[z, other, 1] + zr_p[3, other].astype(F32) + zr_m[3, other].astype(F32)).astype(BF16)
    last_sem = next(sems)
    send_in(last_s, last_r, last_sem, pair, z)
    sent.append(lambda: sent_in(last_s, last_sem, pair, z))
    hop(0, 2, 0, True)
    hop(0, 2, 1, False)
    pair_sum(5)
    hop(0, 3, 1, True)
    pair_sum(6)
    hop(0, 3, 0, False)
    hop(0, 3, 0, True)
    hop(0, 3, 1, False)
    full[half:2 * half] = own[z, yb, 1] + zr_p[3, yb].astype(F32) + zr_m[3, yb].astype(F32)
    recv_in(last_r, last_sem, pair, z)
    full[half:2 * half] = full[half:2 * half] + last_r[...].astype(F32)
    pair_sum(7)
    for h in (1, 0):
        recv_in(yr_p.at[3, h], up_sem[(0, 3, h)], up_z, z)
        recv_in(yr_m.at[3, h], down_sem[(0, 3, h)], down_z, z)
    for h in (0, 1):
        full[h * quarter:(h + 1) * quarter] = (
            own[z, yb, 0, h * quarter:(h + 1) * quarter] + yr_p[3, h].astype(F32) + yr_m[3, h].astype(F32)
        )

    def gelu(value):
        return (0.5 * value * (1.0 + lax.erf(value * math.sqrt(0.5)))).astype(BF16)

    def hidden(size):
        acts[yb, z, :, 0:size] = gelu(full[:, 0:size])

    def attention(size):
        acts[yb, z, :, HEAD:size] = gelu(full[:, 3 * HEAD:5 * HEAD])
        query = full[:, 0:HEAD].astype(BF16)
        keyed = full[:, HEAD:2 * HEAD].astype(BF16)
        valued = full[:, 2 * HEAD:3 * HEAD].astype(BF16)
        scores = lax.dot_general(query, keyed, (((1,), (1,)), ((), ())), preferred_element_type=F32)
        scores = scores * (1.0 / math.sqrt(HEAD))
        expo = jnp.exp(scores - jnp.max(scores, axis=-1, keepdims=True))
        probs = (expo / jnp.sum(expo, axis=-1, keepdims=True)).astype(BF16)
        acts[yb, z, :, 0:HEAD] = jnp.dot(probs, valued, preferred_element_type=F32).astype(BF16)

    is_wide = wide(z)
    pl.when(is_wide)(lambda: hidden(wide_mix))
    pl.when(jnp.logical_not(is_wide))(lambda: attention(narrow_mix))

    def view(image, block, lo, hi, w):
        return acts.at[image, block, lo:hi, 0:w]

    def send_act(image, block, lo, hi, sem, device):
        by_width(block, narrow_mix, wide_mix, lambda w: remote(
            view(image, block, lo, hi, w), view(image, block, lo, hi, w), sem, device).start())
        sent.append(lambda: by_width(block, narrow_mix, wide_mix, lambda w: remote(
            view(image, block, lo, hi, w), view(image, block, lo, hi, w), sem, device).wait_send()))

    def recv_act(image, block, lo, hi, sem, device):
        by_width(block, narrow_mix, wide_mix, lambda w: remote(
            view(image, block, lo, hi, w), view(image, block, lo, hi, w), sem, device).wait_recv())

    images = [yb, other, yb]
    spans = [(0, half), (0, half), (half, 2 * half)]
    gather_sem = {}

    def pass_on(stage, stream, upward):
        lo, hi = spans[stream]
        if stage == 3:
            mid = lo + quarter
            lo, hi = (lo, mid) if upward else (mid, hi)
        block = around(-stage) if upward else around(stage)
        sem = next(sems)
        gather_sem[(stage, stream, upward)] = sem
        send_act(images[stream], block, lo, hi, sem, up_z if upward else down_z)

    def arrived(stage, stream, upward):
        lo, hi = spans[stream]
        if stage == 3:
            mid = lo + quarter
            lo, hi = (lo, mid) if upward else (mid, hi)
        block = around(-1 - stage) if upward else around(1 + stage)
        recv_act(images[stream], block, lo, hi, gather_sem[(stage, stream, upward)], up_z if upward else down_z)
        return block, lo, hi

    pair_first = next(sems)
    send_act(yb, z, 0, half, pair_first, pair)
    for stream in (0, 2):
        pass_on(0, stream, True)
        pass_on(0, stream, False)
    pair_waits = []
    own_sem = next(sems)
    send_act(yb, z, half, 2 * half, own_sem, pair)
    pair_waits.append((z, half, 2 * half, own_sem))
    recv_act(other, z, 0, half, pair_first, pair)
    pass_on(0, 1, True)
    pass_on(0, 1, False)

    for copy, kind in weight_waits:
        if kind == 1:
            copy.wait()

    def add_product(image, block, lo, hi):
        def add(w):
            acc[image, lo:hi] = acc[image, lo:hi] + jnp.dot(
                acts[image, block, lo:hi, 0:w], w_mix[block, 0:w], preferred_element_type=F32)
        by_width(block, narrow_mix, wide_mix, add)

    def add_block(block):
        add_product(0, block, 0, 2 * half)
        add_product(1, block, 0, 2 * half)

    acc[...] = jnp.zeros_like(acc)
    for stage in range(4):
        for stream in (0, 2, 1):
            for upward in (True, False):
                block, lo, hi = arrived(stage, stream, upward)
                if stage < 3:
                    pass_on(stage + 1, stream, upward)
                if stream == 2:
                    sem = next(sems)
                    send_act(yb, block, lo, hi, sem, pair)
                    pair_waits.append((block, lo, hi, sem))
    for block, lo, hi, sem in pair_waits:
        recv_act(other, block, lo, hi, sem, pair)

    def block_products(i, carry):
        add_block(i)
        return carry

    lax.fori_loop(0, NZ, block_products, 0)

    mix_s[...] = acc[...].astype(BF16).reshape(2, n_col, patches, feats)
    mix_copies = []
    for step in range(1, n_col):
        target = lax.rem(col + step, n_col)
        copy = remote(mix_s.at[:, target], mix_r.at[step - 1], next(sems), {"col": target})
        copy.start()
        mix_copies.append(copy)
    total = x_ref[...].astype(F32) + mix_s[:, col].astype(F32)
    for step, copy in enumerate(mix_copies):
        copy.wait()
        total = total + mix_r[step].astype(F32)
    y_ref[...] = total.astype(BF16)
    for wait in sent:
        wait()


def layer(x, weights):
    gain, wq, wk, wv, wup, wout, wdown = weights
    n_col = lax.axis_size("col")
    images, patches, feats = x.shape
    half = n_col // 2 * patches
    wide_in = 6 * HEAD
    vmem = pl.BlockSpec(memory_space=pltpu.VMEM)
    anywhere = pl.BlockSpec(memory_space=pl.ANY)
    z_buf = pltpu.VMEM((4, 2, half, wide_in), BF16)
    y_buf = pltpu.VMEM((4, 2, half // 2, wide_in), BF16)
    pair_buf = pltpu.VMEM((NZ, half, wide_in), BF16)
    scratch = [
        pltpu.VMEM((NZ, feats, wide_in), BF16),
        pltpu.VMEM((NZ, wide_in, feats), BF16),
        pltpu.VMEM((2, n_col, patches, feats), BF16),
        pltpu.VMEM((NZ, 2, 2, half, wide_in), F32),
        pltpu.VMEM((2 * NZ, 8, 128), F32),
        z_buf, z_buf, z_buf, z_buf, y_buf, y_buf, y_buf, y_buf, pair_buf, pair_buf,
        pltpu.VMEM((half, wide_in), BF16), pltpu.VMEM((half, wide_in), BF16),
        pltpu.VMEM((2 * half, wide_in), F32),
        pltpu.VMEM((2, NZ, 2 * half, wide_in), BF16),
        pltpu.VMEM((2, 2 * half, feats), F32),
        pltpu.VMEM((2, n_col, patches, feats), BF16),
        pltpu.VMEM((n_col - 1, 2, patches, feats), BF16),
        pltpu.SemaphoreType.DMA((40,)),
        pltpu.SemaphoreType.DMA((128,)),
        pltpu.SemaphoreType.DMA((128,)),
    ]
    return pl.pallas_call(
        functools.partial(layer_kernel, n_col, patches, feats),
        out_shape=jax.ShapeDtypeStruct(x.shape, BF16),
        in_specs=[vmem, vmem] + [anywhere] * 6,
        out_specs=vmem,
        scratch_shapes=scratch,
        compiler_params=pltpu.CompilerParams(
            collective_id=0, has_side_effects=True, vmem_limit_bytes=60 * 1024 * 1024
        ),
    )(x, gain[None], wq, wk, wv, wup, wout, wdown)


def local(tokens, ln_gain, w_query, w_key, w_value, w_up, w_out, w_down):
    weights = (ln_gain[0], w_query[0], w_key[0], w_value[0], w_up[0], w_out[0], w_down[0])
    section = lax.axis_index("section")
    sections = lax.axis_size("section")
    result = jnp.zeros_like(tokens)
    current = tokens
    for tick in range(sections):
        output = layer(current, weights)
        result = jnp.where(section == tick, output, result)
        if tick + 1 < sections:
            current = lax.ppermute(output, "section", [(s, s + 1) for s in range(sections - 1)])
    return result[None]


def solution(mesh):
    return jax.shard_map(
        local,
        mesh=mesh,
        in_specs=(
            P(None, "col", "row"),
            P("section", "row"),
            P("section", "row", "col"),
            P("section", "row", "col"),
            P("section", "row", "col"),
            P("section", "row", "col"),
            P("section", "col", "row"),
            P("section", "col", "row"),
        ),
        out_specs=P("section", None, "col", "row"),
        check_vma=False,
    )
```

time: 578 us -> 226 us (0.39)
  waiting for transfers between devices: 357 us -> 5.23 us
  Pallas kernels: 0 us -> 217 us
  blocking collectives: 127 us -> 0 us
  starting transfers between devices: 23.4 us -> 1.29 us
  matrix products: 20.8 us -> 0 us
  local copies, waits for them, and re-layouts: 16.8 us -> 0.62 us
  other arithmetic: 16.1 us -> 1.44 us
  between operations: 13.8 us -> 0.05 us
    pallas_call x0 -> x2, Pallas kernels: none -> 217 us  [layer(): pl.pallas_call(functools.partial(layer_kernel, n_col, patches, feats), ou...]
    all_gather x4 -> x0, waiting for transfers between devices: 201 us -> none  [the longest x2 131 us: in_one_piece(): filled = lax.all_gather(both, axis, axis=dim, tiled=True)]
    reduce_scatter x2 -> x0, waiting for transfers between devices: 137 us -> none  [sent_together(): filled = lax.psum_scatter(both, axis, scatter_dimension=dim, tiled=True)]
    all_gather x2 -> x0, blocking collectives: 65.6 us -> none  [layer(): lax.all_gather(attn, 'row', axis=1, tiled=True)]
    all_to_all x4 -> x0, blocking collectives: 61.1 us -> none  [the longest x3 40.1 us: copy_for_each(): return lax.all_to_all(copies, axis, split_axis=0, concat_axis=0, tiled=True)]
    all_to_all x2 -> x0, starting transfers between devices: 21.6 us -> none  [the longest x1 12.6 us: summed_on_arrival(): lax.all_to_all(tiles, axis, split_axis=0, concat_axis=0, tiled=True)]
    dot_general x14 -> x0, matrix products: 20.1 us -> none  [the longest x2 8.91 us: layer(): jnp.dot(act_full, wdown, preferred_element_type=jnp.float32)]
    all_to_all x2 -> x0, waiting for transfers between devices: 14.2 us -> none  [the longest x1 7.7 us: summed_on_arrival(): lax.all_to_all(tiles, axis, split_axis=0, concat_axis=0, tiled=True)]
  transfers between devices with their start and end apart: 9 -> 1, of which waited for: 9 -> 1; matrix products, arithmetic and copies ran while one was open for 4% -> 0% of each run, Pallas kernels for 0% -> 0%
where the time goes in v1:
time: 226 us
  Pallas kernels  217 us (96%)
  waiting for transfers between devices  5.23 us (2%)
    pallas_call x2, Pallas kernels, layer(): pl.pallas_call(functools.partial(layer_kernel, n_col, patches, feats), ou...  217 us
    ppermute x1, waiting for transfers between devices, local(): lax.ppermute(output, 'section', [(s, s + 1) for s in range(sections - 1)])  5.23 us
  transfers between devices with their start and end apart: 1, of which 1 were waited for; matrix products, arithmetic and copies ran while one was open for 0% of the time, Pallas kernels for 0%

profile of v1, /device:TPU:17, one launch (start us, length us, event | category | flops | bytes accessed | tf_op | source)
XLA Modules:
  0.0 226.1 jit_solution(12542454246146742891)
XLA Ops:
  0.0 111.0 %shard_map.82 = bf16[2,32,384]{2,1,0:T(8,128)(2,1)} custom-call(bf16[2,32,384]{2,1,0:T(8,128)(2,1)} %x_ref.1, f32[1,384]{1,0:T(1,128)} %gain_ref.3, bf16[384,768]{1,0:T(8,128)(2,1)} %bitcast.12, bf16[384,768]{1,0:T(8,128)(2,1)} %bitcast.14, bf16[384,768]{1,0:T(8,128)(2,1)} %bitcast.16, bf16[384,3072]{1,0:T(8,128)(2,1)} %bitcast.8, ...), custom_call_target="tpu_custom_call" | custom-call | tf_op jit(solution)/shard_map/pallas_call | solution.py:438
  111.0 1.3 collective-permute-start
  112.3 0.0 copy-start
  112.3 5.2 %collective-permute-done.x_ref = bf16[2,32,384]{2,1,0:T(8,128)(2,1)S(1)} collective-permute-done((bf16[2,32,384]{2,1,0:T(8,128)(2,1)}, bf16[2,32,384]{2,1,0:T(8,128)(2,1)S(1)}, u32[]{:S(2)}, u32[]{:S(2)}) %collective-permute-start) | collective-permute-done | bytes 49184 | tf_op jit(solution)/shard_map/ppermute | solution.py:460
  117.6 0.0 copy-start.1
  117.6 0.6 copy-done.1
  118.2 106.4 %shard_map.83 = bf16[2,32,384]{2,1,0:T(8,128)(2,1)} custom-call(bf16[2,32,384]{2,1,0:T(8,128)(2,1)} %copy-done.1, f32[1,384]{1,0:T(1,128)} %gain_ref.3, bf16[384,768]{1,0:T(8,128)(2,1)} %bitcast.13, bf16[384,768]{1,0:T(8,128)(2,1)} %bitcast.15, bf16[384,768]{1,0:T(8,128)(2,1)} %bitcast.17, bf16[384,3072]{1,0:T(8,128)(2,1)} %bitcast.9, ...), custom_call_target="tpu_custom_call" | custom-call | tf_op jit(solution)/shard_map/pallas_call | solution.py:438
  224.6 0.0 copy-done
  224.6 1.4 select_bitcast_fusion
Async XLA Ops:
  111.0 6.5 %collective-permute-start = (bf16[2,32,384]{2,1,0:T(8,128)(2,1)}, bf16[2,32,384]{2,1,0:T(8,128)(2,1)S(1)}, u32[]{:S(2)}, u32[]{:S(2)}) collective-permute-start(bf16[2,32,384]{2,1,0:T(8,128)(2,1)} %shard_map.82), channel_id=1, source_target_pairs={{0,128},{1,129},{2,130},{3,131},{4,132},{5,133},{6,134},{7,135},{8... | collective-permute-start | bytes 147464 | tf_op jit(solution)/shard_map/ppermute | solution.py:460
  112.3 112.3 %copy-start = (bf16[2,32,384]{2,1,0:T(8,128)(2,1)S(1)}, bf16[2,32,384]{2,1,0:T(8,128)(2,1)}, u32[]{:S(2)}) copy-start(bf16[2,32,384]{2,1,0:T(8,128)(2,1)} %shard_map.82) | copy-start | bytes 147460
  117.6 0.6 copy-start.1

commit v2 on v0

v2 whole, which is shorter than its diff:
```python
import functools
import math

import jax
import jax.numpy as jnp
from jax import lax
from jax.experimental import pallas as pl
from jax.experimental.pallas import tpu as pltpu
from jax.sharding import PartitionSpec as P

D = 6144
HEAD = 128
EPS = 1e-06
NZ = 8
MESH = pl.DeviceIdType.MESH
BF16 = jnp.bfloat16
F32 = jnp.float32


def wide(block):
    return lax.rem(block, 4) == 3


def by_width(block, narrow_size, wide_size, action):
    is_wide = wide(block)

    @pl.when(is_wide)
    def _():
        action(wide_size)

    @pl.when(jnp.logical_not(is_wide))
    def _():
        action(narrow_size)


def layers_kernel(
    n_col, patches, feats,
    x_ref, gain_ref, wq_ref, wk_ref, wv_ref, wup_ref, wout_ref, wdn_ref,
    y_ref,
    w_in, w_mix, gathered, own, stat,
    zs_p, zs_m, zr_p, zr_m, ys_p, ys_m, yr_p, yr_m, pair_s, pair_r, last_s, last_r,
    full, acts, acc, mix_s, mix_r,
    w1_in, w1_mix, gain1, xb1, gathered1, own1, stat1, zs1_p, zs1_m, zr1_p, zr1_m,
    acts1, acc1, mix1_s, mix1_r, ys1, yr1,
    w_sem, ssem, rsem,
):
    section = lax.axis_index("section")
    row = lax.axis_index("row")
    col = lax.axis_index("col")
    n_row = 2 * NZ
    yb = lax.div(row, NZ)
    z = lax.rem(row, NZ)
    other = 1 - yb

    def around(step):
        return lax.rem(z + step + NZ, NZ)

    up_z = {"row": yb * NZ + around(1)}
    down_z = {"row": yb * NZ + around(-1)}
    pair = {"row": other * NZ + z}
    outer = {"section": 1 - section, "row": other * NZ + z}
    diagonal = {"section": 1 - section, "row": row}
    in_first = section == 0
    in_second = section == 1

    narrow_in, wide_in = 5 * HEAD, 6 * HEAD
    narrow_mix, wide_mix = 3 * HEAD, 6 * HEAD
    half = n_col // 2 * patches
    quarter = half // 2

    barrier = pltpu.get_barrier_semaphore()
    for step in range(1, n_row):
        pl.semaphore_signal(barrier, inc=1, device_id={"row": lax.rem(row + step, n_row)}, device_id_type=MESH)
    for step in range(1, n_col):
        pl.semaphore_signal(barrier, inc=1, device_id={"col": lax.rem(col + step, n_col)}, device_id_type=MESH)
    for device in (outer, diagonal):
        pl.semaphore_signal(barrier, inc=1, device_id=device, device_id_type=MESH)

    sems = iter(range(1000))

    def remote(source, target, sem, device):
        return pltpu.make_async_remote_copy(
            src_ref=source, dst_ref=target, send_sem=ssem.at[sem], recv_sem=rsem.at[sem],
            device_id=device, device_id_type=MESH,
        )

    def ready():
        pl.semaphore_wait(barrier, n_row - 1 + n_col - 1 + 2)

    def column_stats(sums, squares):
        columns = jnp.concatenate(
            [jnp.broadcast_to(sums, (2 * patches, 128)), jnp.broadcast_to(squares, (2 * patches, 128))], axis=0
        )
        return columns.T[0:8]

    def mean_and_scale(total):
        mean = total * (1.0 / D)
        lane = lax.broadcasted_iota(jnp.int32, (8, 128), 1)
        shifted = pltpu.roll(mean, 2 * patches, axis=1)
        var = jnp.maximum(mean - shifted * shifted, 0.0)
        both = jnp.where(lane < 2 * patches, mean, lax.rsqrt(var + EPS))
        back = jnp.broadcast_to(both[0:1], (128, 128)).T
        return back[0:2 * patches, 0:1], back[2 * patches:4 * patches, 0:1]

    def gelu(value):
        return (0.5 * value * (1.0 + lax.erf(value * math.sqrt(0.5)))).astype(BF16)

    def attend(query, keyed, valued):
        scores = lax.dot_general(query, keyed, (((1,), (1,)), ((), ())), preferred_element_type=F32)
        scores = scores * (1.0 / math.sqrt(HEAD))
        expo = jnp.exp(scores - jnp.max(scores, axis=-1, keepdims=True))
        probs = (expo / jnp.sum(expo, axis=-1, keepdims=True)).astype(BF16)
        return jnp.dot(probs, valued, preferred_element_type=F32).astype(BF16)

    group = feats
    block_sems = {name: [next(sems) for _ in range(n)] for name, n in
                  (("pair", 5), ("outer", 5), ("via", 5), ("forward", 5), ("gain", 3))}
    mlp_first = 2 * group
    mlp_rest = 3 * group

    def head_cols(member, j):
        return pl.ds(pl.multiple_of((member * 3 + j) * HEAD, HEAD), HEAD)

    def third(at, g):
        return w_in.at[at + g // 2, :, (g % 2) * group:(g % 2 + 1) * group]

    @pl.when(in_second)
    def ship():
        copies = []

        def fetch(source, target):
            copy = pltpu.make_async_copy(source, target, w_sem.at[len(copies)])
            copy.start()
            copies.append(copy)

        start = pl.multiple_of(mlp_first + yb * mlp_rest, group)
        fetch(wup_ref.at[:, pl.ds(start, 2 * group)], w_in.at[4])
        fetch(wup_ref.at[:, pl.ds(pl.multiple_of(start + 2 * group, group), group)], w_in.at[5, :, 0:group])
        fetch(wdn_ref.at[pl.ds(start, 2 * group)], w_mix.at[3])
        fetch(wdn_ref.at[pl.ds(pl.multiple_of(start + 2 * group, group), group)], w_mix.at[4, 0:group])
        n_via = len(copies)
        start = pl.multiple_of(mlp_first + other * mlp_rest, group)
        fetch(wup_ref.at[:, pl.ds(start, 2 * group)], w_in.at[2])
        fetch(wup_ref.at[:, pl.ds(pl.multiple_of(start + 2 * group, group), group)], w_in.at[3, :, 0:group])
        fetch(wdn_ref.at[pl.ds(start, 2 * group)], w_mix.at[1])
        fetch(wdn_ref.at[pl.ds(pl.multiple_of(start + 2 * group, group), group)], w_mix.at[2, 0:group])
        n_outer = len(copies)
        for member, mine in ((other, False), (yb, True)):
            for j in range(3):
                for k, w_ref in enumerate((wq_ref, wk_ref, wv_ref)):
                    span = slice(k * HEAD, (k + 1) * HEAD)
                    at = (j % 2) * group + k * HEAD
                    target = w1_in.at[j, yb, :, span] if mine else w_in.at[j // 2, :, at:at + HEAD]
                    fetch(w_ref.at[:, head_cols(member, j)], target)
            rows = pl.ds(pl.multiple_of(member * group, group), group)
            fetch(wup_ref.at[:, rows], w1_in.at[3, yb] if mine else w_in.at[1, :, group:2 * group])
            fetch(wout_ref.at[rows], w1_mix.at[yb, 0:group] if mine else w_mix.at[0, 0:group])
            fetch(wdn_ref.at[rows], w1_mix.at[yb, group:2 * group] if mine else w_mix.at[0, group:2 * group])
            if not mine:
                n_pair = len(copies)
        gain1[yb] = jnp.broadcast_to(gain_ref[...], (8, feats))
        ready()
        out = []

        def send(source, target, sem, device):
            copy = remote(source, target, sem, device)
            copy.start()
            out.append(copy)

        for copy in copies[:n_via]:
            copy.wait()
        for g in range(3):
            send(third(4, g), third(6, g), block_sems["via"][g], pair)
        send(w_mix.at[3], w_mix.at[5], block_sems["via"][3], pair)
        send(w_mix.at[4, 0:group], w_mix.at[6, 0:group], block_sems["via"][4], pair)
        for copy in copies[n_via:n_outer]:
            copy.wait()
        for g in range(3):
            send(third(2, g), w1_in.at[g, yb], block_sems["outer"][g], outer)
        send(w_mix.at[1], w1_mix.at[yb, 0:2 * group], block_sems["outer"][3], outer)
        send(w_mix.at[2, 0:group], w1_mix.at[yb, 2 * group:3 * group], block_sems["outer"][4], outer)
        for copy in copies[n_outer:n_pair]:
            copy.wait()
        for g in range(4):
            send(third(0, g), w1_in.at[g, yb], block_sems["pair"][g], pair)
        send(w_mix.at[0], w1_mix.at[yb, 0:2 * group], block_sems["pair"][4], pair)
        for device, sem in zip((pair, outer, diagonal), block_sems["gain"]):
            send(gain1.at[yb], gain1.at[yb], sem, device)
        for g in range(3):
            remote(third(6, g), third(6, g), block_sems["via"][g], pair).wait_recv()
            send(third(6, g), w1_in.at[g, other], block_sems["forward"][g], outer)
        remote(w_mix.at[5], w_mix.at[5], block_sems["via"][3], pair).wait_recv()
        send(w_mix.at[5], w1_mix.at[other, 0:2 * group], block_sems["forward"][3], outer)
        remote(w_mix.at[6, 0:group], w_mix.at[6, 0:group], block_sems["via"][4], pair).wait_recv()
        send(w_mix.at[6, 0:group], w1_mix.at[other, 2 * group:3 * group], block_sems["forward"][4], outer)
        for copy in copies[n_pair:]:
            copy.wait()
        for g in range(4):
            remote(w1_in.at[g, other], w1_in.at[g, other], block_sems["pair"][g], pair).wait_recv()
        remote(w1_mix.at[other, 0:2 * group], w1_mix.at[other, 0:2 * group], block_sems["pair"][4], pair).wait_recv()
        remote(gain1.at[other], gain1.at[other], block_sems["gain"][0], pair).wait_recv()
        for copy in out:
            copy.wait_send()

    def first_layer():
        sent = []
        weight_waits = []
        for block in range(NZ):
            if block % 4 == 3:
                start = 6 * 2 * HEAD + (block // 4) * wide_in
                copies_in = [(wup_ref.at[:, start:start + wide_in], 0, wide_in)]
                copies_out = [(wdn_ref.at[start:start + wide_mix], 0, wide_mix)]
            else:
                head = block - block // 4
                cols = slice(head * HEAD, (head + 1) * HEAD)
                start = head * 2 * HEAD
                copies_in = [
                    (wq_ref.at[:, cols], 0, HEAD),
                    (wk_ref.at[:, cols], HEAD, HEAD),
                    (wv_ref.at[:, cols], 2 * HEAD, HEAD),
                    (wup_ref.at[:, start:start + 2 * HEAD], 3 * HEAD, 2 * HEAD),
                ]
                copies_out = [
                    (wout_ref.at[cols], 0, HEAD),
                    (wdn_ref.at[start:start + 2 * HEAD], HEAD, 2 * HEAD),
                ]
            for source, at, size in copies_in:
                copy = pltpu.make_async_copy(source, w_in.at[block, :, at:at + size], w_sem.at[len(weight_waits)])
                copy.start()
                weight_waits.append((copy, 0))
            for source, at, size in copies_out:
                copy = pltpu.make_async_copy(source, w_mix.at[block, at:at + size], w_sem.at[len(weight_waits)])
                copy.start()
                weight_waits.append((copy, 1))

        xf = x_ref[...].astype(F32).reshape(2 * patches, feats)
        sums = jnp.sum(xf, axis=-1, keepdims=True)
        squares = jnp.sum(xf * xf, axis=-1, keepdims=True)
        stat[row] = column_stats(sums, squares)
        ready()
        stat_copies = []
        for step in range(1, n_row):
            copy = remote(stat.at[row], stat.at[row], next(sems), {"row": lax.rem(row + step, n_row)})
            copy.start()
            stat_copies.append(copy)
        for copy in stat_copies:
            copy.wait()
        mean, scale = mean_and_scale(jnp.sum(stat[...], axis=0))
        normed = (xf - mean) * scale * gain_ref[...]
        gathered[:, col] = normed.astype(BF16).reshape(2, patches, feats)
        col_copies = []
        for step in range(1, n_col):
            copy = remote(gathered.at[:, col], gathered.at[:, col], next(sems), {"col": lax.rem(col + step, n_col)})
            copy.start()
            col_copies.append(copy)
        for copy, kind in weight_waits:
            if kind == 0:
                copy.wait()
        for copy in col_copies:
            copy.wait()

        first_up, first_down = next(sems), next(sems)
        early_up, early_down = next(sems), next(sems)
        pair_base = next(sems)
        for _ in range(NZ - 1):
            next(sems)

        def send_in(source, target, sem, device, block):
            by_width(block, narrow_in, wide_in,
                     lambda w: remote(source.at[:, 0:w], target.at[:, 0:w], sem, device).start())

        def recv_in(target, sem, device, block):
            by_width(block, narrow_in, wide_in,
                     lambda w: remote(target.at[:, 0:w], target.at[:, 0:w], sem, device).wait_recv())

        def sent_in(source, sem, device, block):
            by_width(block, narrow_in, wide_in,
                     lambda w: remote(source.at[:, 0:w], source.at[:, 0:w], sem, device).wait_send())


        def order(i):
            away = 4 - lax.div(i + 1, 2)
            return around(jnp.where(lax.rem(i, 2) == 1, away, -away))

        def product(i, carry):
            block = order(i)
            own[block] = jnp.dot(gathered[...].reshape(2 * n_col * patches, feats), w_in[block],
                                 preferred_element_type=F32).reshape(2, 2, half, wide_in)
            pair_s[i] = own[block, other, 0].astype(BF16)

            @pl.when(i == 0)
            def _():
                zs_p[0, 0] = own[block, 0, 1].astype(BF16)
                send_in(zs_p.at[0, 0], zr_p.at[0, 0], first_up, up_z, block)
                zs_m[0, 1] = own[block, 1, 1].astype(BF16)
                send_in(zs_m.at[0, 1], zr_m.at[0, 1], first_down, down_z, block)

            @pl.when(i == 1)
            def _():
                zs_p[1, 1] = own[block, 1, 1].astype(BF16)
                send_in(zs_p.at[1, 1], zr_p.at[1, 1], early_up, up_z, block)

            @pl.when(i == 2)
            def _():
                zs_m[1, 0] = own[block, 0, 1].astype(BF16)
                send_in(zs_m.at[1, 0], zr_m.at[1, 0], early_down, down_z, block)

            send_in(pair_s.at[i], pair_r.at[i], pair_base + i, pair, block)
            return carry

        lax.fori_loop(0, NZ, product, 0)
        for i in range(NZ):
            sent.append(lambda i=i: sent_in(pair_s.at[i], pair_base + i, pair, order(jnp.int32(i))))

        def up_block(stage):
            return around(4 - stage)

        def down_block(stage):
            return around(stage - 4)

        up_sem = {(1, 0, 0): first_up, (1, 1, 1): early_up}
        down_sem = {(1, 0, 1): first_down, (1, 1, 0): early_down}
        for key in [(1, 0, 0), (1, 1, 1)]:
            sent.append(lambda key=key: sent_in(zs_p.at[key[1], key[2]], up_sem[key], up_z, up_block(key[1])))
        for key in [(1, 0, 1), (1, 1, 0)]:
            sent.append(lambda key=key: sent_in(zs_m.at[key[1], key[2]], down_sem[key], down_z, down_block(key[1])))

        def mine(which, h, block):
            if which == 1:
                return own[block, h, 1]
            rows = slice(h * quarter, (h + 1) * quarter)
            return own[block, yb, 0, rows]

        def hop(which, stage, h, upward, extra=None):
            send_buf = (zs_p if upward else zs_m) if which == 1 else (ys_p if upward else ys_m)
            recv_buf = (zr_p if upward else zr_m) if which == 1 else (yr_p if upward else yr_m)
            table = up_sem if upward else down_sem
            device = up_z if upward else down_z
            source_device = device
            block = up_block(stage) if upward else down_block(stage)
            value = mine(which, h, block) if extra is None else extra
            first_half = 0 if upward else 1
            has_arrival = stage >= 2 or (stage == 1 and h == first_half)
            if has_arrival:
                recv_in(recv_buf.at[stage - 1, h], table[(which, stage - 1, h)], source_device, block)
                value = value + recv_buf[stage - 1, h].astype(F32)
            send_buf[stage, h] = value.astype(BF16)
            sem = next(sems)
            table[(which, stage, h)] = sem
            send_in(send_buf.at[stage, h], recv_buf.at[stage, h], sem, device, block)
            sent.append(lambda: sent_in(send_buf.at[stage, h], sem, device, block))

        hop(1, 1, 0, True)
        hop(1, 1, 1, False)

        def pair_sum(i):
            block = order(jnp.int32(i))
            recv_in(pair_r.at[i], pair_base + i, pair, block)
            own[block, yb, 0] = own[block, yb, 0] + pair_r[i].astype(F32)

        for stage in (2, 3):
            hop(1, stage, 1, True)
            hop(1, stage, 0, False)
            if stage == 2:
                pair_sum(0)
                hop(0, 0, 0, True)
                hop(0, 0, 1, False)
            hop(1, stage, 0, True)
            hop(1, stage, 1, False)
            if stage == 2:
                pair_sum(1)
                hop(0, 1, 1, True)
                pair_sum(2)
                hop(0, 1, 0, False)
        hop(0, 1, 0, True)
        hop(0, 1, 1, False)
        pair_sum(3)
        hop(0, 2, 1, True)
        pair_sum(4)
        hop(0, 2, 0, False)
        for h in (1, 0):
            recv_in(zr_p.at[3, h], up_sem[(1, 3, h)], up_z, z)
            recv_in(zr_m.at[3, h], down_sem[(1, 3, h)], down_z, z)
        last_s[...] = (own[z, other, 1] + zr_p[3, other].astype(F32) + zr_m[3, other].astype(F32)).astype(BF16)
        last_sem = next(sems)
        send_in(last_s, last_r, last_sem, pair, z)
        sent.append(lambda: sent_in(last_s, last_sem, pair, z))
        hop(0, 2, 0, True)
        hop(0, 2, 1, False)
        pair_sum(5)
        hop(0, 3, 1, True)
        pair_sum(6)
        hop(0, 3, 0, False)
        hop(0, 3, 0, True)
        hop(0, 3, 1, False)
        full[half:2 * half] = own[z, yb, 1] + zr_p[3, yb].astype(F32) + zr_m[3, yb].astype(F32)
        recv_in(last_r, last_sem, pair, z)
        full[half:2 * half] = full[half:2 * half] + last_r[...].astype(F32)
        pair_sum(7)
        for h in (1, 0):
            recv_in(yr_p.at[3, h], up_sem[(0, 3, h)], up_z, z)
            recv_in(yr_m.at[3, h], down_sem[(0, 3, h)], down_z, z)
        for h in (0, 1):
            full[h * quarter:(h + 1) * quarter] = (
                own[z, yb, 0, h * quarter:(h + 1) * quarter] + yr_p[3, h].astype(F32) + yr_m[3, h].astype(F32)
            )

        def hidden(size):
            acts[yb, z, :, 0:size] = gelu(full[:, 0:size])

        def attention(size):
            acts[yb, z, :, HEAD:size] = gelu(full[:, 3 * HEAD:5 * HEAD])
            acts[yb, z, :, 0:HEAD] = attend(
                full[:, 0:HEAD].astype(BF16), full[:, HEAD:2 * HEAD].astype(BF16), full[:, 2 * HEAD:3 * HEAD].astype(BF16)
            )

        is_wide = wide(z)
        pl.when(is_wide)(lambda: hidden(wide_mix))
        pl.when(jnp.logical_not(is_wide))(lambda: attention(narrow_mix))

        def view(image, block, lo, hi, w):
            return acts.at[image, block, lo:hi, 0:w]

        def send_act(image, block, lo, hi, sem, device):
            by_width(block, narrow_mix, wide_mix, lambda w: remote(
                view(image, block, lo, hi, w), view(image, block, lo, hi, w), sem, device).start())
            sent.append(lambda: by_width(block, narrow_mix, wide_mix, lambda w: remote(
                view(image, block, lo, hi, w), view(image, block, lo, hi, w), sem, device).wait_send()))

        def recv_act(image, block, lo, hi, sem, device):
            by_width(block, narrow_mix, wide_mix, lambda w: remote(
                view(image, block, lo, hi, w), view(image, block, lo, hi, w), sem, device).wait_recv())

        images = [yb, other, yb]
        spans = [(0, half), (0, half), (half, 2 * half)]
        gather_sem = {}

        def pass_on(stage, stream, upward):
            lo, hi = spans[stream]
            if stage == 3:
                mid = lo + quarter
                lo, hi = (lo, mid) if upward else (mid, hi)
            block = around(-stage) if upward else around(stage)
            sem = next(sems)
            gather_sem[(stage, stream, upward)] = sem
            send_act(images[stream], block, lo, hi, sem, up_z if upward else down_z)

        def arrived(stage, stream, upward):
            lo, hi = spans[stream]
            if stage == 3:
                mid = lo + quarter
                lo, hi = (lo, mid) if upward else (mid, hi)
            block = around(-1 - stage) if upward else around(1 + stage)
            recv_act(images[stream], block, lo, hi, gather_sem[(stage, stream, upward)], up_z if upward else down_z)
            return block, lo, hi

        pair_first = next(sems)
        send_act(yb, z, 0, half, pair_first, pair)
        for stream in (0, 2):
            pass_on(0, stream, True)
            pass_on(0, stream, False)
        pair_waits = []
        own_sem = next(sems)
        send_act(yb, z, half, 2 * half, own_sem, pair)
        pair_waits.append((z, half, 2 * half, own_sem))
        recv_act(other, z, 0, half, pair_first, pair)
        pass_on(0, 1, True)
        pass_on(0, 1, False)

        for copy, kind in weight_waits:
            if kind == 1:
                copy.wait()

        def add_product(image, block, lo, hi):
            def add(w):
                acc[image, lo:hi] = acc[image, lo:hi] + jnp.dot(
                    acts[image, block, lo:hi, 0:w], w_mix[block, 0:w], preferred_element_type=F32)
            by_width(block, narrow_mix, wide_mix, add)

        def add_block(block):
            add_product(0, block, 0, 2 * half)
            add_product(1, block, 0, 2 * half)

        acc[...] = jnp.zeros_like(acc)
        for stage in range(4):
            for stream in (0, 2, 1):
                for upward in (True, False):
                    block, lo, hi = arrived(stage, stream, upward)
                    if stage < 3:
                        pass_on(stage + 1, stream, upward)
                    if stream == 2:
                        sem = next(sems)
                        send_act(yb, block, lo, hi, sem, pair)
                        pair_waits.append((block, lo, hi, sem))
        for block, lo, hi, sem in pair_waits:
            recv_act(other, block, lo, hi, sem, pair)

        def block_products(i, carry):
            add_block(i)
            return carry

        lax.fori_loop(0, NZ, block_products, 0)

        mix_s[...] = acc[...].astype(BF16).reshape(2, n_col, patches, feats)
        mix_copies = []
        for step in range(1, n_col):
            target = lax.rem(col + step, n_col)
            copy = remote(mix_s.at[:, target], mix_r.at[step - 1], next(sems), {"col": target})
            copy.start()
            mix_copies.append(copy)
        total = x_ref[...].astype(F32) + mix_s[:, col].astype(F32)
        for step, copy in enumerate(mix_copies):
            copy.wait()
            total = total + mix_r[step].astype(F32)
        y_ref[...] = total.astype(BF16)
        xb1[yb] = total.astype(BF16)
        for device, sem in ((pair, spread[0]), (outer, spread[1]), (diagonal, spread[2])):
            copy = remote(xb1.at[yb], xb1.at[yb], sem, device)
            copy.start()
            sent.append(copy.wait_send)
        for wait in sent:
            wait()
        for g in range(3):
            remote(w1_in.at[g, other], w1_in.at[g, other], block_sems["outer"][g], outer).wait_recv()
            remote(w1_in.at[g, yb], w1_in.at[g, yb], block_sems["forward"][g], outer).wait_recv()
        for half_k, name in ((other, "outer"), (yb, "forward")):
            for k, (lo, hi) in ((3, (0, 2 * group)), (4, (2 * group, 3 * group))):
                part = w1_mix.at[half_k, lo:hi]
                remote(part, part, block_sems[name][k], outer).wait_recv()
        remote(gain1.at[other], gain1.at[other], block_sems["gain"][1], outer).wait_recv()
        remote(gain1.at[yb], gain1.at[yb], block_sems["gain"][2], diagonal).wait_recv()
        remote(xb1.at[other], xb1.at[other], spread[0], pair).wait_recv()

    spread = [next(sems) for _ in range(3)]
    pl.when(in_first)(first_layer)

    @pl.when(in_second)
    def _():
        remote(xb1.at[other], xb1.at[other], spread[1], outer).wait_recv()
        remote(xb1.at[yb], xb1.at[yb], spread[2], diagonal).wait_recv()

    sent = []
    n_tok = 2 * n_col * patches
    both = xb1[...].astype(F32).reshape(2, 2 * patches, feats)
    sums = jnp.sum(jnp.sum(both, axis=-1, keepdims=True), axis=0)
    squares = jnp.sum(jnp.sum(both * both, axis=-1, keepdims=True), axis=0)
    stat1[z] = column_stats(sums, squares)
    copies = []
    for step in range(1, NZ):
        copy = remote(stat1.at[z], stat1.at[z], next(sems), {"row": yb * NZ + around(step)})
        copy.start()
        copies.append(copy)
    for copy in copies:
        copy.wait()
    mean, scale = mean_and_scale(jnp.sum(stat1[...], axis=0))
    for k in range(2):
        normed = (both[k] - mean) * scale * gain1[k, 0:1]
        gathered1[k, :, col] = normed.astype(BF16).reshape(2, patches, feats)
    copies = []
    for step in range(1, n_col):
        copy = remote(gathered1.at[:, :, col], gathered1.at[:, :, col], next(sems), {"col": lax.rem(col + step, n_col)})
        copy.start()
        copies.append(copy)
    for copy in copies:
        copy.wait()

    half_rows = 4 * patches
    short_rows = 3 * patches

    def partial_product(g):
        return (
            jnp.dot(gathered1[0].reshape(n_tok, feats), w1_in[g, 0], preferred_element_type=F32)
            + jnp.dot(gathered1[1].reshape(n_tok, feats), w1_in[g, 1], preferred_element_type=F32)
        )

    @pl.when(in_first)
    def _():
        for g in range(3):
            value = partial_product(g).reshape(NZ, 2, patches, group)
            own1[:, :, g * patches:(g + 1) * patches] = value

    @pl.when(in_second)
    def _():
        for g in range(4):
            value = partial_product(g).reshape(2, 2, half_rows, group)
            own1[g] = value[0]
            own1[4 + g] = value[1]

    def by_section(action):
        pl.when(in_first)(lambda: action(short_rows))
        pl.when(in_second)(lambda: action(half_rows))

    up1, down1 = {}, {}

    def hop1(stage, h, upward):
        send_buf, recv_buf = (zs1_p, zr1_p) if upward else (zs1_m, zr1_m)
        table = up1 if upward else down1
        device = up_z if upward else down_z
        block = around(4 - stage) if upward else around(stage - 4)
        value = own1[block, h]
        if stage >= 2 or (stage == 1 and h == (0 if upward else 1)):
            sem = table[(stage - 1, h)]
            by_section(lambda n: remote(
                recv_buf.at[stage - 1, h, 0:n], recv_buf.at[stage - 1, h, 0:n], sem, device).wait_recv())
            value = value + recv_buf[stage - 1, h].astype(F32)
        send_buf[stage, h] = value.astype(BF16)
        sem_out = next(sems)
        table[(stage, h)] = sem_out
        by_section(lambda n: remote(
            send_buf.at[stage, h, 0:n], recv_buf.at[stage, h, 0:n], sem_out, device).start())
        sent.append(lambda: by_section(lambda n: remote(
            send_buf.at[stage, h, 0:n], recv_buf.at[stage, h, 0:n], sem_out, device).wait_send()))

    hop1(0, 0, True)
    hop1(0, 1, False)
    for stage in (1, 2, 3):
        hop1(stage, 1, True)
        hop1(stage, 0, False)
        hop1(stage, 0, True)
        hop1(stage, 1, False)
    for h in (1, 0):
        by_section(lambda n: remote(zr1_p.at[3, h, 0:n], zr1_p.at[3, h, 0:n], up1[(3, h)], up_z).wait_recv())
        by_section(lambda n: remote(zr1_m.at[3, h, 0:n], zr1_m.at[3, h, 0:n], down1[(3, h)], down_z).wait_recv())

    def summed(h):
        return own1[z, h] + zr1_p[3, h].astype(F32) + zr1_m[3, h].astype(F32)

    has_head = jnp.logical_and(in_second, jnp.logical_not(wide(z)))

    @pl.when(has_head)
    def _():
        value = jnp.concatenate([summed(0), summed(1)], axis=0).astype(BF16)
        result = attend(value[:, 0:HEAD], value[:, HEAD:2 * HEAD], value[:, 2 * HEAD:3 * HEAD])
        acts1[z, :, :, 0:HEAD] = result.reshape(2, half_rows, HEAD)

    @pl.when(jnp.logical_not(has_head))
    def _():
        for h in range(2):
            acts1[z, h] = gelu(summed(h))

    def by_kind(block, action):
        pl.when(in_first)(lambda: action(short_rows, group))
        is_wide = wide(block)
        pl.when(jnp.logical_and(in_second, is_wide))(lambda: action(half_rows, group))
        pl.when(jnp.logical_and(in_second, jnp.logical_not(is_wide)))(lambda: action(half_rows, HEAD))

    gather1 = {}

    def pass_on1(stage, h, upward):
        block = around(-stage) if upward else around(stage)
        sem = next(sems)
        gather1[(stage, h, upward)] = sem
        device = up_z if upward else down_z

        def copy(n, w):
            part = acts1.at[block, h, 0:n, 0:w]
            return remote(part, part, sem, device)

        by_kind(block, lambda n, w: copy(n, w).start())
        sent.append(lambda: by_kind(block, lambda n, w: copy(n, w).wait_send()))

    def arrived1(stage, h, upward):
        block = around(-1 - stage) if upward else around(1 + stage)
        device = up_z if upward else down_z
        by_kind(block, lambda n, w: remote(
            acts1.at[block, h, 0:n, 0:w], acts1.at[block, h, 0:n, 0:w], gather1[(stage, h, upward)], device).wait_recv())

    for h in range(2):
        for upward in (True, False):
            pass_on1(0, h, upward)
    for stage in range(4):
        for h in range(2):
            for upward in (True, False):
                if stage == 3 and h != (0 if upward else 1):
                    continue
                arrived1(stage, h, upward)
                if stage < 2 or (stage == 2 and h == (0 if upward else 1)):
                    pass_on1(stage + 1, h, upward)

    @pl.when(in_first)
    def _():
        for k in range(2):
            total = None
            for g in range(3):
                hidden = acts1[:, :, g * patches:(g + 1) * patches].reshape(n_tok, group)
                term = jnp.dot(hidden, w1_mix[k, g * group:(g + 1) * group], preferred_element_type=F32)
                total = term if total is None else total + term
            acc1[k] = total

    @pl.when(in_second)
    def _():
        for image in range(2):
            first = image * 4
            value = jnp.concatenate(
                [acts1[first + j, :, :, 0:HEAD].reshape(2 * half_rows, HEAD) for j in range(3)]
                + [acts1[first + 3].reshape(2 * half_rows, group)], axis=1)
            for k in range(2):
                acc1[k, image * 2 * half_rows:(image + 1) * 2 * half_rows] = jnp.dot(
                    value, w1_mix[k, 0:2 * group], preferred_element_type=F32)

    for k in range(2):
        mix1_s[k] = acc1[k].astype(BF16).reshape(2, n_col, patches, feats)
    copies = []
    for step in range(1, n_col):
        target = lax.rem(col + step, n_col)
        copy = remote(mix1_s.at[:, :, target], mix1_r.at[step - 1], next(sems), {"col": target})
        copy.start()
        copies.append(copy)
    total = mix1_s[:, :, col].astype(F32)
    for step, copy in enumerate(copies):
        copy.wait()
        total = total + mix1_r[step].astype(F32)
    ys1[...] = total.astype(BF16)
    to_pair, to_outer, to_diagonal = next(sems), next(sems), next(sems)

    @pl.when(in_first)
    def _():
        copies = [remote(ys1.at[other], yr1.at[1], to_outer, outer), remote(ys1.at[yb], yr1.at[2], to_diagonal, diagonal)]
        for copy in copies:
            copy.start()
        for copy in copies:
            copy.wait_send()

    @pl.when(in_second)
    def _():
        copy = remote(ys1.at[other], yr1.at[0], to_pair, pair)
        copy.start()
        copy.wait()
        remote(yr1.at[1], yr1.at[1], to_outer, outer).wait_recv()
        remote(yr1.at[2], yr1.at[2], to_diagonal, diagonal).wait_recv()
        result = xb1[yb].astype(F32) + ys1[yb].astype(F32)
        for k in range(3):
            result = result + yr1[k].astype(F32)
        y_ref[...] = result.astype(BF16)

    assert next(sems) < 208
    for wait in sent:
        wait()


def layers(x, weights):
    gain, wq, wk, wv, wup, wout, wdown = weights
    n_col = lax.axis_size("col")
    images, patches, feats = x.shape
    half = n_col // 2 * patches
    wide_in = 6 * HEAD
    vmem = pl.BlockSpec(memory_space=pltpu.VMEM)
    anywhere = pl.BlockSpec(memory_space=pl.ANY)
    z_buf = pltpu.VMEM((4, 2, half, wide_in), BF16)
    y_buf = pltpu.VMEM((4, 2, half // 2, wide_in), BF16)
    z1_buf = pltpu.VMEM((4, 2, 4 * patches, feats), BF16)
    pair_buf = pltpu.VMEM((NZ, half, wide_in), BF16)
    scratch = [
        pltpu.VMEM((NZ, feats, wide_in), BF16),
        pltpu.VMEM((NZ, wide_in, feats), BF16),
        pltpu.VMEM((2, n_col, patches, feats), BF16),
        pltpu.VMEM((NZ, 2, 2, half, wide_in), F32),
        pltpu.VMEM((2 * NZ, 8, 128), F32),
        z_buf, z_buf, z_buf, z_buf, y_buf, y_buf, y_buf, y_buf, pair_buf, pair_buf,
        pltpu.VMEM((half, wide_in), BF16), pltpu.VMEM((half, wide_in), BF16),
        pltpu.VMEM((2 * half, wide_in), F32),
        pltpu.VMEM((2, NZ, 2 * half, wide_in), BF16),
        pltpu.VMEM((2, 2 * half, feats), F32),
        pltpu.VMEM((2, n_col, patches, feats), BF16),
        pltpu.VMEM((n_col - 1, 2, patches, feats), BF16),
        pltpu.VMEM((4, 2, feats, feats), BF16),
        pltpu.VMEM((2, 3 * feats, feats), BF16),
        pltpu.VMEM((2, 8, feats), F32),
        pltpu.VMEM((2, 2, patches, feats), BF16),
        pltpu.VMEM((2, 2, n_col, patches, feats), BF16),
        pltpu.VMEM((NZ, 2, 4 * patches, feats), F32),
        pltpu.VMEM((NZ, 8, 128), F32),
        z1_buf, z1_buf, z1_buf, z1_buf,
        pltpu.VMEM((NZ, 2, 4 * patches, feats), BF16),
        pltpu.VMEM((2, 2 * n_col * patches, feats), F32),
        pltpu.VMEM((2, 2, n_col, patches, feats), BF16),
        pltpu.VMEM((n_col - 1, 2, 2, patches, feats), BF16),
        pltpu.VMEM((2, 2, patches, feats), BF16),
        pltpu.VMEM((3, 2, patches, feats), BF16),
        pltpu.SemaphoreType.DMA((40,)),
        pltpu.SemaphoreType.DMA((208,)),
        pltpu.SemaphoreType.DMA((208,)),
    ]
    return pl.pallas_call(
        functools.partial(layers_kernel, n_col, patches, feats),
        out_shape=jax.ShapeDtypeStruct(x.shape, BF16),
        in_specs=[vmem, vmem] + [anywhere] * 6,
        out_specs=vmem,
        scratch_shapes=scratch,
        compiler_params=pltpu.CompilerParams(
            collective_id=0, has_side_effects=True, vmem_limit_bytes=67043328
        ),
    )(x, gain[None], wq, wk, wv, wup, wout, wdown)


def local(tokens, ln_gain, w_query, w_key, w_value, w_up, w_out, w_down):
    weights = (ln_gain[0], w_query[0], w_key[0], w_value[0], w_up[0], w_out[0], w_down[0])
    return layers(tokens, weights)[None]


def solution(mesh):
    return jax.shard_map(
        local,
        mesh=mesh,
        in_specs=(
            P(None, "col", "row"),
            P("section", "row"),
            P("section", "row", "col"),
            P("section", "row", "col"),
            P("section", "row", "col"),
            P("section", "row", "col"),
            P("section", "col", "row"),
            P("section", "col", "row"),
        ),
        out_specs=P("section", None, "col", "row"),
        check_vma=False,
    )
```

time: 578 us -> 181 us (0.31)
  waiting for transfers between devices: 357 us -> 0 us
  Pallas kernels: 0 us -> 179 us
  blocking collectives: 127 us -> 0 us
  starting transfers between devices: 23.4 us -> 0 us
  matrix products: 20.8 us -> 0 us
  other arithmetic: 16.1 us -> 0 us
  local copies, waits for them, and re-layouts: 16.8 us -> 1.42 us
  between operations: 13.8 us -> 0.01 us
    all_gather x4 -> x0, waiting for transfers between devices: 201 us -> none  [the longest x2 131 us: in_one_piece(): filled = lax.all_gather(both, axis, axis=dim, tiled=True)]
    pallas_call x0 -> x1, Pallas kernels: none -> 179 us  [layers(): pl.pallas_call(functools.partial(layers_kernel, n_col, patches, feats), o...]
    reduce_scatter x2 -> x0, waiting for transfers between devices: 137 us -> none  [sent_together(): filled = lax.psum_scatter(both, axis, scatter_dimension=dim, tiled=True)]
    all_gather x2 -> x0, blocking collectives: 65.6 us -> none  [layer(): lax.all_gather(attn, 'row', axis=1, tiled=True)]
    all_to_all x4 -> x0, blocking collectives: 61.1 us -> none  [the longest x3 40.1 us: copy_for_each(): return lax.all_to_all(copies, axis, split_axis=0, concat_axis=0, tiled=True)]
    all_to_all x2 -> x0, starting transfers between devices: 21.6 us -> none  [the longest x1 12.6 us: summed_on_arrival(): lax.all_to_all(tiles, axis, split_axis=0, concat_axis=0, tiled=True)]
    dot_general x14 -> x0, matrix products: 20.1 us -> none  [the longest x2 8.91 us: layer(): jnp.dot(act_full, wdown, preferred_element_type=jnp.float32)]
    all_to_all x2 -> x0, waiting for transfers between devices: 14.2 us -> none  [the longest x1 7.7 us: summed_on_arrival(): lax.all_to_all(tiles, axis, split_axis=0, concat_axis=0, tiled=True)]
  transfers between devices with their start and end apart: 9 -> 0, of which waited for: 9 -> 0; matrix products, arithmetic and copies ran while one was open for 4% -> 0% of each run, Pallas kernels for 0% -> 0%
where the time goes in v2:
time: 181 us
  Pallas kernels  179 us (99%)
    pallas_call x1, Pallas kernels, layers(): pl.pallas_call(functools.partial(layers_kernel, n_col, patches, feats), o...  179 us

profile of v2, /device:TPU:17, one launch (start us, length us, event | category | flops | bytes accessed | tf_op | source)
XLA Modules:
  0.0 180.8 jit_solution(593910304284413352)
XLA Ops:
  0.0 179.4 %shard_map.82 = bf16[2,32,384]{2,1,0:T(8,128)(2,1)} custom-call(bf16[2,32,384]{2,1,0:T(8,128)(2,1)} %x_ref.1, f32[1,384]{1,0:T(1,128)} %gain_ref.1, bf16[384,768]{1,0:T(8,128)(2,1)} %bitcast.9, bf16[384,768]{1,0:T(8,128)(2,1)} %bitcast.10, bf16[384,768]{1,0:T(8,128)(2,1)} %bitcast.11, bf16[384,3072]{1,0:T(8,128)(2,1)} %bitcast.7, bf16[768,384]{1,0:T(8,128)(2,1)} %bitcast.12, ...), custom_call_target="tpu_custom_call" | custom-call | tf_op jit(solution)/shard_map/pallas_call | solution.py:784
  179.4 1.4 copy.10

commit v3 on v2

--- a/solution.py
+++ b/solution.py
@@ -39,9 +39,10 @@
     y_ref,
     w_in, w_mix, gathered, own, stat,
     zs_p, zs_m, zr_p, zr_m, ys_p, ys_m, yr_p, yr_m, pair_s, pair_r, last_s, last_r,
-    full, acts, acc, mix_s, mix_r,
+    full, acts, acc, mix_s,
+    stat_col, mix_d, mix_t,
     w1_in, w1_mix, gain1, xb1, gathered1, own1, stat1, zs1_p, zs1_m, zr1_p, zr1_m,
-    acts1, acc1, mix1_s, mix1_r, ys1, yr1,
+    acts1, acc1, mix1_s, mix_r, ys1, yr1,
     w_sem, ssem, rsem,
 ):
     section = lax.axis_index("section")
@@ -60,6 +61,16 @@
     pair = {"row": other * NZ + z}
     outer = {"section": 1 - section, "row": other * NZ + z}
     diagonal = {"section": 1 - section, "row": row}
+    n_x = n_col // 2
+    core = lax.rem(col, 2)
+    chip_x = lax.div(col, 2)
+    sibling = {"col": 2 * chip_x + 1 - core}
+
+    def along_x(step):
+        return lax.rem(chip_x + step, n_x)
+
+    def same_core(step):
+        return {"col": 2 * along_x(step) + core}
     in_first = section == 0
     in_second = section == 1
 
@@ -93,14 +104,43 @@
         )
         return columns.T[0:8]
 
-    def mean_and_scale(total):
+    def lane_stats(total):
         mean = total * (1.0 / D)
         lane = lax.broadcasted_iota(jnp.int32, (8, 128), 1)
         shifted = pltpu.roll(mean, 2 * patches, axis=1)
         var = jnp.maximum(mean - shifted * shifted, 0.0)
-        both = jnp.where(lane < 2 * patches, mean, lax.rsqrt(var + EPS))
-        back = jnp.broadcast_to(both[0:1], (128, 128)).T
-        return back[0:2 * patches, 0:1], back[2 * patches:4 * patches, 0:1]
+        return jnp.where(lane < 2 * patches, mean, lax.rsqrt(var + EPS))
+
+    def to_columns(table):
+        rows = table[:, 0, :]
+        return jnp.concatenate([rows] * (128 // n_col), axis=0).T
+
+    def normalise(block, columns, c, gain):
+        value = block.astype(F32).reshape(2 * patches, feats)
+        mean, scale = columns[0:2 * patches, c:c + 1], columns[2 * patches:4 * patches, c:c + 1]
+        return ((value - mean) * scale * gain).astype(BF16).reshape(2, patches, feats)
+
+    def col_gather(view):
+        arrive = []
+        for step in (1, 3, 2):
+            copy = remote(view(col), view(col), next(sems), same_core(step))
+            copy.start()
+            arrive.append((copy, step))
+        first = remote(view(col), view(col), next(sems), sibling)
+        first.start()
+
+        def finish():
+            handed = [first]
+            for copy, step in arrive:
+                copy.wait()
+                block = view(2 * along_x(n_x - step) + core)
+                onward = remote(block, block, next(sems), sibling)
+                onward.start()
+                handed.append(onward)
+            for copy in handed:
+                copy.wait()
+
+        return finish
 
     def gelu(value):
         return (0.5 * value * (1.0 + lax.erf(value * math.sqrt(0.5)))).astype(BF16)
@@ -111,6 +151,27 @@
         expo = jnp.exp(scores - jnp.max(scores, axis=-1, keepdims=True))
         probs = (expo / jnp.sum(expo, axis=-1, keepdims=True)).astype(BF16)
         return jnp.dot(probs, valued, preferred_element_type=F32).astype(BF16)
+
+    def col_sum(parts, from_sibling, sums, arrived_sums, at, read):
+        swap = remote(at(parts, slice(None), 1 - core), at(from_sibling), next(sems), sibling)
+        swap.start()
+        swap.wait()
+        out = []
+        for step in (2, 1, 3):
+            target = along_x(step)
+            value = read(parts, target, core).astype(F32) + read(from_sibling, target).astype(F32)
+            put(sums, at, target, value.astype(BF16))
+            copy = remote(at(sums, target), at(arrived_sums.at[step - 1]), next(sems), same_core(step))
+            copy.start()
+            out.append((copy, step))
+        value = read(parts, chip_x, core).astype(F32) + read(from_sibling, chip_x).astype(F32)
+        for copy, step in out:
+            copy.wait()
+            value = value + read(arrived_sums.at[step - 1]).astype(F32)
+        return value
+
+    def put(ref, at, target, value):
+        at(ref, target)[...] = value
 
     group = feats
     block_sems = {name: [next(sems) for _ in range(n)] for name, n in
@@ -238,26 +299,25 @@
         squares = jnp.sum(xf * xf, axis=-1, keepdims=True)
         stat[row] = column_stats(sums, squares)
         ready()
+        gathered[:, col] = x_ref[...]
         stat_copies = []
         for step in range(1, n_row):
             copy = remote(stat.at[row], stat.at[row], next(sems), {"row": lax.rem(row + step, n_row)})
             copy.start()
             stat_copies.append(copy)
+        finish_x = col_gather(lambda c: gathered.at[:, c])
         for copy in stat_copies:
             copy.wait()
-        mean, scale = mean_and_scale(jnp.sum(stat[...], axis=0))
-        normed = (xf - mean) * scale * gain_ref[...]
-        gathered[:, col] = normed.astype(BF16).reshape(2, patches, feats)
-        col_copies = []
-        for step in range(1, n_col):
-            copy = remote(gathered.at[:, col], gathered.at[:, col], next(sems), {"col": lax.rem(col + step, n_col)})
-            copy.start()
-            col_copies.append(copy)
+        stat_col[0, col] = lane_stats(jnp.sum(stat[...], axis=0))
+        finish_stats = col_gather(lambda c: stat_col.at[0, c])
         for copy, kind in weight_waits:
             if kind == 0:
                 copy.wait()
-        for copy in col_copies:
-            copy.wait()
+        finish_x()
+        finish_stats()
+        columns = to_columns(stat_col[0])
+        for c in range(n_col):
+            gathered[:, c] = normalise(gathered[:, c], columns, c, gain_ref[...])
 
         first_up, first_down = next(sems), next(sems)
         early_up, early_down = next(sems), next(sems)
@@ -459,10 +519,8 @@
         for stream in (0, 2):
             pass_on(0, stream, True)
             pass_on(0, stream, False)
-        pair_waits = []
         own_sem = next(sems)
         send_act(yb, z, half, 2 * half, own_sem, pair)
-        pair_waits.append((z, half, 2 * half, own_sem))
         recv_act(other, z, 0, half, pair_first, pair)
         pass_on(0, 1, True)
         pass_on(0, 1, False)
@@ -477,13 +535,26 @@
                     acts[image, block, lo:hi, 0:w], w_mix[block, 0:w], preferred_element_type=F32)
             by_width(block, narrow_mix, wide_mix, add)
 
-        def add_block(block):
-            add_product(0, block, 0, 2 * half)
-            add_product(1, block, 0, 2 * half)
-
         acc[...] = jnp.zeros_like(acc)
+        pair_done = {}
+
+        def products_of(stage):
+            for block in sorted_blocks(stage):
+                add_product(yb, block, 0, 2 * half)
+                add_product(other, block, 0, half)
+
+        def sorted_blocks(stage):
+            return [around(1 + stage)] if stage == 3 else [around(1 + stage), around(-1 - stage)]
+
+        def pair_products(waits, blocks):
+            for wait in waits:
+                recv_act(other, *wait, pair)
+            for block in blocks:
+                add_product(other, block, half, 2 * half)
+
         for stage in range(4):
-            for stream in (0, 2, 1):
+            coming = []
+            for stream in (2, 0, 1):
                 for upward in (True, False):
                     block, lo, hi = arrived(stage, stream, upward)
                     if stage < 3:
@@ -491,27 +562,20 @@
                     if stream == 2:
                         sem = next(sems)
                         send_act(yb, block, lo, hi, sem, pair)
-                        pair_waits.append((block, lo, hi, sem))
-        for block, lo, hi, sem in pair_waits:
-            recv_act(other, block, lo, hi, sem, pair)
-
-        def block_products(i, carry):
-            add_block(i)
-            return carry
-
-        lax.fori_loop(0, NZ, block_products, 0)
-
-        mix_s[...] = acc[...].astype(BF16).reshape(2, n_col, patches, feats)
-        mix_copies = []
-        for step in range(1, n_col):
-            target = lax.rem(col + step, n_col)
-            copy = remote(mix_s.at[:, target], mix_r.at[step - 1], next(sems), {"col": target})
-            copy.start()
-            mix_copies.append(copy)
-        total = x_ref[...].astype(F32) + mix_s[:, col].astype(F32)
-        for step, copy in enumerate(mix_copies):
-            copy.wait()
-            total = total + mix_r[step].astype(F32)
+                        coming.append((block, lo, hi, sem))
+            pair_done[stage] = coming
+            if stage == 0:
+                add_product(yb, z, 0, 2 * half)
+                add_product(other, z, 0, half)
+                pair_products([(z, half, 2 * half, own_sem)], [z])
+            else:
+                pair_products(pair_done[stage - 1], sorted_blocks(stage - 1))
+            products_of(stage)
+        pair_products(pair_done[3], sorted_blocks(3))
+        mix_s[...] = acc[...].astype(BF16).reshape(2, n_x, 2, patches, feats)
+        total = x_ref[...].astype(F32) + col_sum(
+            mix_s, mix_d.at[0], mix_t.at[0], mix_r.at[:, 0], lambda ref, *at: ref.at[(slice(None), *at)],
+            lambda ref, *at: ref[(slice(None), *at)])
         y_ref[...] = total.astype(BF16)
         xb1[yb] = total.astype(BF16)
         for device, sem in ((pair, spread[0]), (outer, spread[1]), (diagonal, spread[2])):
@@ -550,19 +614,19 @@
         copy = remote(stat1.at[z], stat1.at[z], next(sems), {"row": yb * NZ + around(step)})
         copy.start()
         copies.append(copy)
+    for k in range(2):
+        gathered1[k, :, col] = xb1[k]
+    finish_x1 = col_gather(lambda c: gathered1.at[:, :, c])
     for copy in copies:
         copy.wait()
-    mean, scale = mean_and_scale(jnp.sum(stat1[...], axis=0))
-    for k in range(2):
-        normed = (both[k] - mean) * scale * gain1[k, 0:1]
-        gathered1[k, :, col] = normed.astype(BF16).reshape(2, patches, feats)
-    copies = []
-    for step in range(1, n_col):
-        copy = remote(gathered1.at[:, :, col], gathered1.at[:, :, col], next(sems), {"col": lax.rem(col + step, n_col)})
-        copy.start()
-        copies.append(copy)
-    for copy in copies:
-        copy.wait()
+    stat_col[1, col] = lane_stats(jnp.sum(stat1[...], axis=0))
+    finish_stats1 = col_gather(lambda c: stat_col.at[1, c])
+    finish_x1()
+    finish_stats1()
+    columns1 = to_columns(stat_col[1])
+    for c in range(n_col):
+        for k in range(2):
+            gathered1[k, :, c] = normalise(gathered1[k, :, c], columns1, c, gain1[k, 0:1])
 
     half_rows = 4 * patches
     short_rows = 3 * patches
@@ -699,17 +763,11 @@
                     value, w1_mix[k, 0:2 * group], preferred_element_type=F32)
 
     for k in range(2):
-        mix1_s[k] = acc1[k].astype(BF16).reshape(2, n_col, patches, feats)
-    copies = []
-    for step in range(1, n_col):
-        target = lax.rem(col + step, n_col)
-        copy = remote(mix1_s.at[:, :, target], mix1_r.at[step - 1], next(sems), {"col": target})
-        copy.start()
-        copies.append(copy)
-    total = mix1_s[:, :, col].astype(F32)
-    for step, copy in enumerate(copies):
-        copy.wait()
-        total = total + mix1_r[step].astype(F32)
+        mix1_s[k] = acc1[k].astype(BF16).reshape(2, n_x, 2, patches, feats)
+    both_dims = (slice(None), slice(None))
+    total = col_sum(
+        mix1_s, mix_d, mix_t, mix_r, lambda ref, *at: ref.at[(*both_dims, *at)],
+        lambda ref, *at: ref[(*both_dims, *at)])
     ys1[...] = total.astype(BF16)
     to_pair, to_outer, to_diagonal = next(sems), next(sems), next(sems)
 
@@ -761,8 +819,10 @@
         pltpu.VMEM((2 * half, wide_in), F32),
         pltpu.VMEM((2, NZ, 2 * half, wide_in), BF16),
         pltpu.VMEM((2, 2 * half, feats), F32),
-        pltpu.VMEM((2, n_col, patches, feats), BF16),
-        pltpu.VMEM((n_col - 1, 2, patches, feats), BF16),
+        pltpu.VMEM((2, n_col // 2, 2, patches, feats), BF16),
+        pltpu.VMEM((2, n_col, 8, 128), F32),
+        pltpu.VMEM((2, 2, n_col // 2, patches, feats), BF16),
+        pltpu.VMEM((2, 2, n_col // 2, patches, feats), BF16),
         pltpu.VMEM((4, 2, feats, feats), BF16),
         pltpu.VMEM((2, 3 * feats, feats), BF16),
         pltpu.VMEM((2, 8, feats), F32),
@@ -773,8 +833,8 @@
         z1_buf, z1_buf, z1_buf, z1_buf,
         pltpu.VMEM((NZ, 2, 4 * patches, feats), BF16),
         pltpu.VMEM((2, 2 * n_col * patches, feats), F32),
-        pltpu.VMEM((2, 2, n_col, patches, feats), BF16),
-        pltpu.VMEM((n_col - 1, 2, 2, patches, feats), BF16),
+        pltpu.VMEM((2, 2, n_col // 2, 2, patches, feats), BF16),
+        pltpu.VMEM((3, 2, 2, patches, feats), BF16),
         pltpu.VMEM((2, 2, patches, feats), BF16),
         pltpu.VMEM((3, 2, patches, feats), BF16),
         pltpu.SemaphoreType.DMA((40,)),

time: 181 us -> 174 us (0.961); the launches traced: 181 us -> 171 us
  Pallas kernels: 179 us -> 170 us
    pallas_call x1, Pallas kernels: 179 us -> 170 us  [layers(): pl.pallas_call(functools.partial(layers_kernel, n_col, patches, feats), o...]
where the time goes in v3:
time: 174 us; the launch traced here: 171 us
  Pallas kernels  170 us (98%)
    pallas_call x1, Pallas kernels, layers(): pl.pallas_call(functools.partial(layers_kernel, n_col, patches, feats), o...  170 us

profile of v3, /device:TPU:17, one launch (start us, length us, event | category | flops | bytes accessed | tf_op | source)
XLA Modules:
  0.0 171.3 jit_solution(1092022678263240144)
XLA Ops:
  0.0 169.9 %shard_map.82 = bf16[2,32,384]{2,1,0:T(8,128)(2,1)} custom-call(bf16[2,32,384]{2,1,0:T(8,128)(2,1)} %x_ref.1, f32[1,384]{1,0:T(1,128)} %gain_ref.1, bf16[384,768]{1,0:T(8,128)(2,1)} %bitcast.9, bf16[384,768]{1,0:T(8,128)(2,1)} %bitcast.10, bf16[384,768]{1,0:T(8,128)(2,1)} %bitcast.11, bf16[384,3072]{1,0:T(8,128)(2,1)} %bitcast.7, bf16[768,384]{1,0:T(8,128)(2,1)} %bitcast.12, ...), custom_call_target="tpu_custom_call" | custom-call | tf_op jit(solution)/shard_map/pallas_call | solution.py:844
  169.9 1.4 copy.10

commit v4 on v3

v4 whole, which is shorter than its diff:
```python
import functools
import math

import jax
import jax.numpy as jnp
from jax import lax
from jax.experimental import pallas as pl
from jax.experimental.pallas import tpu as pltpu
from jax.sharding import PartitionSpec as P

D = 6144
HEAD = 128
EPS = 1e-06
NZ = 8
MESH = pl.DeviceIdType.MESH
BF16 = jnp.bfloat16
F32 = jnp.float32


def wide(block):
    return lax.rem(block, 4) == 3


def either(condition, yes, no):
    def run(action):
        def branch():
            action()

        return branch

    lax.cond(condition, run(yes), run(no))


def by_width(block, narrow_size, wide_size, action):
    either(wide(block), lambda: action(wide_size), lambda: action(narrow_size))


def layers_kernel(
    n_col, patches, feats,
    x_ref, gain_ref, wq_ref, wk_ref, wv_ref, wup_ref, wout_ref, wdn_ref,
    y_ref,
    w_in, w_mix, w_main, w_g, w_gs, w_ms, gathered, gain0, own, own_g, stat,
    gs_p, gs_m, gr_p, gr_m, zs_p, zs_m, zr_p, zr_m, ys_p, ys_m, yr_p, yr_m, pair_s, pair_r, last_s, last_r,
    full, acts, acc,
    stat_col, xraw, terms, mix_d, mix_t, mix_e,
    w1_in, w1_mix, gain1, xb1, gathered1, own1, stat1, zs1_p, zs1_m, zr1_p, zr1_m,
    acts1, acc1, mix1_s, mix_r, ys1, yr1,
    w_sem, ssem, rsem,
):
    section = lax.axis_index("section")
    row = lax.axis_index("row")
    col = lax.axis_index("col")
    n_row = 2 * NZ
    yb = lax.div(row, NZ)
    z = lax.rem(row, NZ)
    other = 1 - yb

    def around(step):
        return lax.rem(z + step + NZ, NZ)

    up_z = {"row": yb * NZ + around(1)}
    down_z = {"row": yb * NZ + around(-1)}
    pair = {"row": other * NZ + z}
    outer = {"section": 1 - section, "row": other * NZ + z}
    diagonal = {"section": 1 - section, "row": row}
    n_x = n_col // 2
    core = lax.rem(col, 2)
    chip_x = lax.div(col, 2)
    sibling = {"col": 2 * chip_x + 1 - core}

    def along_x(step):
        return lax.rem(chip_x + step, n_x)

    def same_core(step):
        return {"col": 2 * along_x(step) + core}
    in_first = section == 0
    in_second = section == 1

    narrow_mix, wide_mix = 3 * HEAD, 6 * HEAD

    barrier = pltpu.get_barrier_semaphore()
    for step in range(1, n_row):
        pl.semaphore_signal(barrier, inc=1, device_id={"row": lax.rem(row + step, n_row)}, device_id_type=MESH)
    for step in range(1, n_col):
        pl.semaphore_signal(barrier, inc=1, device_id={"col": lax.rem(col + step, n_col)}, device_id_type=MESH)
    for device in (outer, diagonal):
        pl.semaphore_signal(barrier, inc=1, device_id=device, device_id_type=MESH)

    sems = iter(range(1000))

    def remote(source, target, sem, device):
        return pltpu.make_async_remote_copy(
            src_ref=source, dst_ref=target, send_sem=ssem.at[sem], recv_sem=rsem.at[sem],
            device_id=device, device_id_type=MESH,
        )

    def ready():
        pl.semaphore_wait(barrier, n_row - 1 + n_col - 1 + 2)

    def column_stats(sums, squares):
        columns = jnp.concatenate(
            [jnp.broadcast_to(sums, (2 * patches, 128)), jnp.broadcast_to(squares, (2 * patches, 128))], axis=0
        )
        return columns.T[0:8]

    def lane_stats(total):
        mean = total * (1.0 / D)
        lane = lax.broadcasted_iota(jnp.int32, (8, 128), 1)
        shifted = pltpu.roll(mean, 2 * patches, axis=1)
        var = jnp.maximum(mean - shifted * shifted, 0.0)
        return jnp.where(lane < 2 * patches, mean, lax.rsqrt(var + EPS))

    def to_columns(table):
        rows = table[:, 0, :]
        return jnp.concatenate([rows] * (128 // n_col), axis=0).T

    def normalise(block, columns, c, gain):
        value = block.astype(F32).reshape(2 * patches, feats)
        mean, scale = columns[0:2 * patches, c:c + 1], columns[2 * patches:4 * patches, c:c + 1]
        return ((value - mean) * scale * gain).astype(BF16).reshape(2, patches, feats)

    def col_gather(view):
        arrive = []
        for step in (1, 3, 2):
            copy = remote(view(col), view(col), next(sems), same_core(step))
            copy.start()
            arrive.append((copy, step))
        first = remote(view(col), view(col), next(sems), sibling)
        first.start()

        def finish():
            handed = [first]
            for copy, step in arrive:
                copy.wait()
                block = view(2 * along_x(n_x - step) + core)
                onward = remote(block, block, next(sems), sibling)
                onward.start()
                handed.append(onward)
            for copy in handed:
                copy.wait()

        return finish

    def gelu(value):
        return (0.5 * value * (1.0 + lax.erf(value * math.sqrt(0.5)))).astype(BF16)

    def attend(query, keyed, valued):
        scores = lax.dot_general(query, keyed, (((1,), (1,)), ((), ())), preferred_element_type=F32)
        scores = scores * (1.0 / math.sqrt(HEAD))
        expo = jnp.exp(scores - jnp.max(scores, axis=-1, keepdims=True))
        probs = (expo / jnp.sum(expo, axis=-1, keepdims=True)).astype(BF16)
        return jnp.dot(probs, valued, preferred_element_type=F32).astype(BF16)

    def col_peers():
        for dx in (2, 1, 3, 0):
            for dc in range(2):
                if dx or dc:
                    target_core = lax.rem(core + dc, 2)
                    yield 2 * dx + dc - 1, along_x(dx), target_core, {"col": 2 * along_x(dx) + target_core}

    def col_direct(view):
        copies = []
        for _, _, _, device in col_peers():
            copy = remote(view(col), view(col), next(sems), device)
            copy.start()
            copies.append(copy)
        return copies

    def col_sum():
        copies = []
        for slot, target_x, target_core, device in col_peers():
            copy = remote(mix1_s.at[:, :, target_x, target_core], mix_r.at[slot], next(sems), device)
            copy.start()
            copies.append((copy, slot))
        value = mix1_s[:, :, chip_x, core].astype(F32)
        for copy, slot in copies:
            copy.wait()
            value = value + mix_r[slot].astype(F32)
        return value

    def col_sum_by_core():
        swap = remote(mix1_s.at[:, :, :, 1 - core], mix_d, next(sems), sibling)
        swap.start()
        swap.wait()
        copies = []
        for step in (2, 1, 3):
            target = along_x(step)
            mix_t[:, :, target] = (
                mix1_s[:, :, target, core].astype(F32) + mix_d[:, :, target].astype(F32)).astype(BF16)
            copy = remote(mix_t.at[:, :, target], mix_e.at[step - 1], next(sems), same_core(step))
            copy.start()
            copies.append((copy, step - 1))
        value = mix1_s[:, :, chip_x, core].astype(F32) + mix_d[:, :, chip_x].astype(F32)
        for copy, slot in copies:
            copy.wait()
            value = value + mix_e[slot].astype(F32)
        return value

    group = feats
    block_sems = {name: [next(sems) for _ in range(n)] for name, n in
                  (("pair", 5), ("outer", 5), ("via", 5), ("forward", 5), ("gain", 3))}
    mlp_first = 2 * group
    mlp_rest = 3 * group

    def head_cols(member, j):
        return pl.ds(pl.multiple_of((member * 3 + j) * HEAD, HEAD), HEAD)

    def third(at, g):
        return w_in.at[at + g // 2, :, (g % 2) * group:(g % 2 + 1) * group]

    @pl.when(in_second)
    def ship():
        copies = []

        def fetch(source, target):
            copy = pltpu.make_async_copy(source, target, w_sem.at[len(copies)])
            copy.start()
            copies.append(copy)

        start = pl.multiple_of(mlp_first + yb * mlp_rest, group)
        fetch(wup_ref.at[:, pl.ds(start, 2 * group)], w_in.at[4])
        fetch(wup_ref.at[:, pl.ds(pl.multiple_of(start + 2 * group, group), group)], w_in.at[5, :, 0:group])
        fetch(wdn_ref.at[pl.ds(start, 2 * group)], w_mix.at[3])
        fetch(wdn_ref.at[pl.ds(pl.multiple_of(start + 2 * group, group), group)], w_mix.at[4, 0:group])
        n_via = len(copies)
        start = pl.multiple_of(mlp_first + other * mlp_rest, group)
        fetch(wup_ref.at[:, pl.ds(start, 2 * group)], w_in.at[2])
        fetch(wup_ref.at[:, pl.ds(pl.multiple_of(start + 2 * group, group), group)], w_in.at[3, :, 0:group])
        fetch(wdn_ref.at[pl.ds(start, 2 * group)], w_mix.at[1])
        fetch(wdn_ref.at[pl.ds(pl.multiple_of(start + 2 * group, group), group)], w_mix.at[2, 0:group])
        n_outer = len(copies)
        for member, mine in ((other, False), (yb, True)):
            for j in range(3):
                for k, w_ref in enumerate((wq_ref, wk_ref, wv_ref)):
                    span = slice(k * HEAD, (k + 1) * HEAD)
                    at = (j % 2) * group + k * HEAD
                    target = w1_in.at[j, yb, :, span] if mine else w_in.at[j // 2, :, at:at + HEAD]
                    fetch(w_ref.at[:, head_cols(member, j)], target)
            rows = pl.ds(pl.multiple_of(member * group, group), group)
            fetch(wup_ref.at[:, rows], w1_in.at[3, yb] if mine else w_in.at[1, :, group:2 * group])
            fetch(wout_ref.at[rows], w1_mix.at[yb, 0:group] if mine else w_mix.at[0, 0:group])
            fetch(wdn_ref.at[rows], w1_mix.at[yb, group:2 * group] if mine else w_mix.at[0, group:2 * group])
            if not mine:
                n_pair = len(copies)
        gain1[yb] = jnp.broadcast_to(gain_ref[...], (8, feats))
        ready()
        out = []

        def send(source, target, sem, device):
            copy = remote(source, target, sem, device)
            copy.start()
            out.append(copy)

        for copy in copies[:n_via]:
            copy.wait()
        for g in range(3):
            send(third(4, g), third(6, g), block_sems["via"][g], pair)
        send(w_mix.at[3], w_mix.at[5], block_sems["via"][3], pair)
        send(w_mix.at[4, 0:group], w_mix.at[6, 0:group], block_sems["via"][4], pair)
        for copy in copies[n_via:n_outer]:
            copy.wait()
        for g in range(3):
            send(third(2, g), w1_in.at[g, yb], block_sems["outer"][g], outer)
        send(w_mix.at[1], w1_mix.at[yb, 0:2 * group], block_sems["outer"][3], outer)
        send(w_mix.at[2, 0:group], w1_mix.at[yb, 2 * group:3 * group], block_sems["outer"][4], outer)
        for copy in copies[n_outer:n_pair]:
            copy.wait()
        for g in range(4):
            send(third(0, g), w1_in.at[g, yb], block_sems["pair"][g], pair)
        send(w_mix.at[0], w1_mix.at[yb, 0:2 * group], block_sems["pair"][4], pair)
        for device, sem in zip((pair, outer, diagonal), block_sems["gain"]):
            send(gain1.at[yb], gain1.at[yb], sem, device)
        for g in range(3):
            remote(third(6, g), third(6, g), block_sems["via"][g], pair).wait_recv()
            send(third(6, g), w1_in.at[g, other], block_sems["forward"][g], outer)
        remote(w_mix.at[5], w_mix.at[5], block_sems["via"][3], pair).wait_recv()
        send(w_mix.at[5], w1_mix.at[other, 0:2 * group], block_sems["forward"][3], outer)
        remote(w_mix.at[6, 0:group], w_mix.at[6, 0:group], block_sems["via"][4], pair).wait_recv()
        send(w_mix.at[6, 0:group], w1_mix.at[other, 2 * group:3 * group], block_sems["forward"][4], outer)
        for copy in copies[n_pair:]:
            copy.wait()
        for g in range(4):
            remote(w1_in.at[g, other], w1_in.at[g, other], block_sems["pair"][g], pair).wait_recv()
        remote(w1_mix.at[other, 0:2 * group], w1_mix.at[other, 0:2 * group], block_sems["pair"][4], pair).wait_recv()
        remote(gain1.at[other], gain1.at[other], block_sems["gain"][0], pair).wait_recv()
        for copy in out:
            copy.wait_send()

    def pieces_of_ring(copy, after=None):
        ring_sem = {}

        def onward(stage, piece, upward):
            block = around(-stage) if upward else around(stage)
            sem = next(sems)
            ring_sem[(stage, piece, upward)] = sem
            copy(block, piece, sem, up_z if upward else down_z, "start")
            sent.append(lambda: copy(block, piece, sem, up_z if upward else down_z, "wait_send"))

        def last(piece, upward):
            return (piece < 2) == upward

        for piece in (2, 3, 0, 1):
            onward(0, piece, True)
            onward(0, (piece + 2) % 4, False)
        if after is not None:
            after(-1)
        for stage in range(4):
            for piece in (2, 3, 0, 1):
                for upward in (True, False):
                    p = piece if upward else (piece + 2) % 4
                    if stage == 3 and not last(p, upward):
                        continue
                    block = around(-1 - stage) if upward else around(1 + stage)
                    copy(block, p, ring_sem[(stage, p, upward)], up_z if upward else down_z, "wait_recv")
                    if stage < 2 or (stage == 2 and last(p, upward)):
                        onward(stage + 1, p, upward)
            if after is not None:
                after(stage)

    sent = []
    main_n, main_w, part_g = 3 * HEAD, 4 * HEAD, 2 * HEAD
    image_rows = n_col * patches
    late = image_rows // 2
    early = image_rows - late
    y_rows = early // 2

    def member_hidden(member, g):
        if g == 3:
            start = 6 * part_g + member * 3 * part_g
            return start, start + main_w
        start = (member * 3 + g) * part_g
        return start, start

    def first_layer():
        waits = {"stage": [], "own": [], "mix": [], "mix_stage": []}
        count = iter(range(1000))

        def fetch(source, target, kind):
            copy = pltpu.make_async_copy(source, target, w_sem.at[next(count)])
            copy.start()
            waits[kind].append(copy)

        def columns_at(start, size):
            return pl.ds(pl.multiple_of(start, HEAD), size)

        for g in range(4):
            fetch(wup_ref.at[:, columns_at(member_hidden(other, g)[1], part_g)], w_gs.at[g], "stage")
        for g in range(4):
            fetch(wup_ref.at[:, columns_at(member_hidden(yb, g)[1], part_g)], w_g.at[g, yb], "own")
        for block in range(NZ):
            member, g = block // 4, block % 4
            if g == 3:
                start = member_hidden(member, g)[0]
                fetch(wup_ref.at[:, start:start + main_w], w_main.at[block], "own")
            else:
                cols = slice((member * 3 + g) * HEAD, (member * 3 + g + 1) * HEAD)
                for k, w_ref in enumerate((wq_ref, wk_ref, wv_ref)):
                    fetch(w_ref.at[:, cols], w_main.at[block, :, k * HEAD:(k + 1) * HEAD], "own")
        for member, kind in ((other, "mix_stage"), (yb, "mix")):
            for g in range(4):
                target = w_ms.at[g] if kind == "mix_stage" else w_mix.at[yb * 4 + g]
                rows = columns_at(member_hidden(member, g)[0], wide_mix if g == 3 else part_g)
                if g == 3:
                    fetch(wdn_ref.at[rows], target, kind)
                else:
                    fetch(wout_ref.at[columns_at((member * 3 + g) * HEAD, HEAD)], target.at[0:HEAD], kind)
                    fetch(wdn_ref.at[rows], target.at[HEAD:narrow_mix], kind)

        xf = x_ref[...].astype(F32).reshape(2 * patches, feats)
        sums = jnp.sum(xf, axis=-1, keepdims=True)
        squares = jnp.sum(xf * xf, axis=-1, keepdims=True)
        stat[row] = column_stats(sums, squares)
        xraw[yb] = x_ref[...]
        gathered[yb, :, col] = x_ref[...]
        gain0[yb] = jnp.broadcast_to(gain_ref[...], (8, feats))
        ready()
        x_copy = remote(xraw.at[yb], xraw.at[yb], x_spread[0], pair)
        x_copy.start()
        stat_copies = []
        for step in range(1, n_row):
            copy = remote(stat.at[row], stat.at[row], next(sems), {"row": lax.rem(row + step, n_row)})
            copy.start()
            stat_copies.append(copy)
        finish_own = col_gather(lambda c: gathered.at[yb, :, c])
        gain_copy = remote(gain0.at[yb], gain0.at[yb], next(sems), pair)
        gain_copy.start()
        for device, sem in ((outer, x_spread[1]), (diagonal, x_spread[2])):
            copy = remote(xraw.at[yb], xraw.at[yb], sem, device)
            copy.start()
            sent.append(copy.wait_send)

        def group_at(i):
            return lax.rem(z + (0, 3, 1, 2)[i], 4)

        def traced_group_at(i):
            return lax.rem(z + jnp.where(i == 0, 0, jnp.where(i == 1, 3, i - 1)), 4)

        g_base = next(sems)
        for _ in range(3):
            next(sems)
        for copy in waits["stage"]:
            copy.wait()
        for i in range(4):
            g = group_at(i)
            copy = remote(w_gs.at[g], w_g.at[g, yb], g_base + i, pair)
            copy.start()
            sent.append(copy.wait_send)
        x_copy.wait()
        gathered[other, :, col] = xraw[other]
        finish_other = col_gather(lambda c: gathered.at[other, :, c])
        finish_own()
        for copy in stat_copies:
            copy.wait()
        stat_col[0, col] = lane_stats(jnp.sum(stat[...], axis=0))
        finish_stats = col_direct(lambda c: stat_col.at[0, c])
        for copy in waits["own"]:
            copy.wait()
        finish_other()
        for copy in finish_stats:
            copy.wait()
        gain_copy.wait()
        columns = to_columns(stat_col[0])
        for c in range(n_col):
            for k in range(2):
                gathered[k, :, c] = normalise(gathered[k, :, c], columns, c, gain0[k, 0:1])

        bufs = {
            "G": (gs_p, gs_m, gr_p, gr_m), "Z": (zs_p, zs_m, zr_p, zr_m), "Y": (ys_p, ys_m, yr_p, yr_m),
        }
        tables = {True: {}, False: {}}
        pair_base = next(sems)
        for _ in range(NZ - 1):
            next(sems)

        def by_part(kind, block, action):
            if kind == "G":
                action(part_g)
            else:
                by_width(block, main_n, main_w, action)

        def move(kind, source, target, sem, device, block, what):
            by_part(kind, block, lambda w: getattr(remote(source.at[:, 0:w], target.at[:, 0:w], sem, device), what)())

        def ring_block(stage, upward):
            return around(4 - stage) if upward else around(stage - 4)

        def term(kind, h, block):
            g, image = lax.rem(block, 4), lax.div(block, 4)
            if kind == "G":
                return own_g[g, image, h]
            if kind == "Z":
                return own[h * 4 + g, image, early:image_rows]
            return own[yb * 4 + g, image, h * y_rows:(h + 1) * y_rows]

        def reserve(kind, stage, h, upward):
            sem = next(sems)
            tables[upward][(kind, stage, h)] = sem
            send_buf = bufs[kind][0 if upward else 1].at[stage, h]
            device = up_z if upward else down_z
            block = ring_block(stage, upward)
            sent.append(lambda: move(kind, send_buf, send_buf, sem, device, block, "wait_send"))

        def hop(kind, stage, h, upward):
            send_buf = bufs[kind][0 if upward else 1]
            recv_buf = bufs[kind][2 if upward else 3]
            device = up_z if upward else down_z
            block = ring_block(stage, upward)
            value = term(kind, h, block)
            if stage >= 2 or (stage == 1 and h == (0 if upward else 1)):
                buf = recv_buf.at[stage - 1, h]
                move(kind, buf, buf, tables[upward][(kind, stage - 1, h)], device, block, "wait_recv")
                value = value + recv_buf[stage - 1, h].astype(F32)
            send_buf[stage, h] = value.astype(BF16)
            if (kind, stage, h) not in tables[upward]:
                reserve(kind, stage, h, upward)
            move(kind, send_buf.at[stage, h], recv_buf.at[stage, h], tables[upward][(kind, stage, h)], device, block, "start")

        for kind in ("G", "Z"):
            reserve(kind, 0, 0, True)
            reserve(kind, 0, 1, False)
            reserve(kind, 1, 1, True)
            reserve(kind, 1, 0, False)

        def order(i):
            away = 4 - lax.div(i + 1, 2)
            return around(jnp.where(lax.rem(i, 2) == 1, away, -away))

        def send_pair(i):
            block = order(i)
            pair_s[i] = own[other * 4 + lax.rem(block, 4), lax.div(block, 4), 0:early].astype(BF16)
            move("Y", pair_s.at[i], pair_r.at[i], pair_base + i, pair, block, "start")

        n_tok = 2 * image_rows

        def product(i, carry):
            g = traced_group_at(i)
            for member in range(2):
                own[member * 4 + g] = jnp.dot(
                    gathered[yb].reshape(n_tok, feats), w_main[member * 4 + g], preferred_element_type=F32
                ).reshape(2, image_rows, main_w)

            @pl.when(i == 0)
            def _():
                hop("Z", 0, 0, True)
                hop("Z", 0, 1, False)

            @pl.when(i == 1)
            def _():
                hop("Z", 1, 1, True)

            @pl.when(i == 2)
            def _():
                hop("Z", 1, 0, False)

            send_pair(i)
            return carry

        def product_g(i, carry):
            g = traced_group_at(i)
            remote(w_g.at[g, other], w_g.at[g, other], g_base + i, pair).wait_recv()
            own_g[g] = (
                jnp.dot(gathered[0].reshape(n_tok, feats), w_g[g, 0], preferred_element_type=F32)
                + jnp.dot(gathered[1].reshape(n_tok, feats), w_g[g, 1], preferred_element_type=F32)
            ).reshape(2, 2, image_rows // 2, part_g)

            @pl.when(i == 0)
            def _():
                hop("G", 0, 0, True)
                hop("G", 0, 1, False)

            @pl.when(i == 1)
            def _():
                hop("G", 1, 1, True)

            @pl.when(i == 2)
            def _():
                hop("G", 1, 0, False)

            return carry

        lax.fori_loop(0, 4, product, 0)

        def rest_of_pair(i, carry):
            send_pair(i)
            return carry

        lax.fori_loop(4, NZ, rest_of_pair, 0)
        for copy in waits["mix_stage"]:
            copy.wait()
        mix_sems = [next(sems) for _ in range(4)]

        def send_mix(g):
            n = wide_mix if g == 3 else narrow_mix
            copy = remote(w_ms.at[g, 0:n], w_mix.at[yb * 4 + g, 0:n], mix_sems[g], pair)
            copy.start()
            sent.append(copy.wait_send)

        for i in range(NZ):
            sent.append(lambda i=i: move(
                "Y", pair_s.at[i], pair_s.at[i], pair_base + i, pair, order(jnp.int32(i)), "wait_send"))

        def pair_sum(i):
            block = order(jnp.int32(i))
            move("Y", pair_r.at[i], pair_r.at[i], pair_base + i, pair, block, "wait_recv")
            at = own.at[yb * 4 + lax.rem(block, 4), lax.div(block, 4), 0:early]
            at[...] = at[...] + pair_r[i].astype(F32)

        def four(kind, stage, before=(None, None)):
            for sums, h, upward in ((before[0], 1, True), (before[1], 0, False), (None, 0, True), (None, 1, False)):
                if sums is not None:
                    pair_sum(sums)
                hop(kind, stage, h, upward)

        def all_in(kind):
            for h, upward in ((1, True), (0, False), (0, True), (1, False)):
                buf = bufs[kind][2 if upward else 3].at[3, h]
                move(kind, buf, buf, tables[upward][(kind, 3, h)], up_z if upward else down_z, z, "wait_recv")

        hop("Z", 1, 0, True)
        hop("Z", 1, 1, False)
        lax.fori_loop(0, 1, product_g, 0)
        four("Z", 2)
        lax.fori_loop(1, 3, product_g, 0)
        four("Z", 3)
        lax.fori_loop(3, 4, product_g, 0)
        hop("G", 1, 0, True)
        hop("G", 1, 1, False)
        pair_sum(0)
        hop("Y", 0, 0, True)
        hop("Y", 0, 1, False)
        four("G", 2)
        all_in("Z")
        last_s[...] = (term("Z", other, z) + zr_p[3, other].astype(F32) + zr_m[3, other].astype(F32)).astype(BF16)
        last_sem = next(sems)
        move("Z", last_s, last_r, last_sem, pair, z, "start")
        sent.append(lambda: move("Z", last_s, last_s, last_sem, pair, z, "wait_send"))
        for g in (3, 0, 1, 2):
            send_mix(g)
        four("Y", 1, (1, 2))
        four("G", 3)
        four("Y", 2, (3, 4))
        four("Y", 3, (5, 6))
        is_wide = wide(z)
        all_in("G")
        for h in range(2):
            hidden = gelu(term("G", h, z) + gr_p[3, h].astype(F32) + gr_m[3, h].astype(F32))

            @pl.when(is_wide)
            def _():
                acts[z, h, :, main_w:wide_mix] = hidden

            @pl.when(jnp.logical_not(is_wide))
            def _():
                acts[z, h, :, HEAD:narrow_mix] = hidden

        full[early:image_rows] = term("Z", yb, z) + zr_p[3, yb].astype(F32) + zr_m[3, yb].astype(F32)
        move("Z", last_r, last_r, last_sem, pair, z, "wait_recv")
        full[early:image_rows] = full[early:image_rows] + last_r[...].astype(F32)
        pair_sum(7)
        all_in("Y")
        for h in range(2):
            full[h * y_rows:(h + 1) * y_rows] = term("Y", h, z) + yr_p[3, h].astype(F32) + yr_m[3, h].astype(F32)

        @pl.when(is_wide)
        def _():
            acts[z, :, :, 0:main_w] = gelu(full[...]).reshape(2, image_rows // 2, main_w)

        @pl.when(jnp.logical_not(is_wide))
        def _():
            value = full[:, 0:main_n].astype(BF16)
            result = attend(value[:, 0:HEAD], value[:, HEAD:2 * HEAD], value[:, 2 * HEAD:3 * HEAD])
            acts[z, :, :, 0:HEAD] = result.reshape(2, image_rows // 2, HEAD)

        piece_rows = image_rows // 4

        def act_copy(block, piece, sem, device, what):
            rows = slice((piece % 2) * piece_rows, (piece % 2 + 1) * piece_rows)

            def action(w):
                part = acts.at[block, piece // 2, rows, 0:w]
                getattr(remote(part, part, sem, device), what)()

            by_width(block, narrow_mix, wide_mix, action)

        def add_product(k, block):
            g, image = lax.rem(block, 4), lax.div(block, 4)

            def add(w):
                acc[k, image] = acc[k, image] + jnp.dot(
                    acts[block, :, :, 0:w].reshape(image_rows, w), w_mix[k * 4 + g, 0:w], preferred_element_type=F32)

            by_width(block, narrow_mix, wide_mix, add)

        def add_known(k, block):
            g, image = block % 4, block // 4
            w = wide_mix if g == 3 else narrow_mix
            acc[k, image] = acc[k, image] + jnp.dot(
                acts[block, :, :, 0:w].reshape(image_rows, w), w_mix[k * 4 + g, 0:w], preferred_element_type=F32)

        acc[...] = jnp.zeros_like(acc)

        def after_stage(stage):
            if stage == -1:
                for copy in waits["mix"]:
                    copy.wait()
                add_product(yb, z)
            elif stage < 3:
                add_product(yb, around(-1 - stage))
                add_product(yb, around(1 + stage))
                if stage == 2:
                    for g in (3, 0, 1, 2):
                        n = wide_mix if g == 3 else narrow_mix
                        part = w_mix.at[other * 4 + g, 0:n]
                        remote(part, part, mix_sems[g], pair).wait_recv()
                        for block in (g, g + 4):
                            pl.when(around(4) != block)(lambda block=block: add_known(other, block))
            else:
                add_product(yb, around(4))
                add_product(other, around(4))

        pieces_of_ring(act_copy, after_stage)

        for k in range(2):
            mix1_s[k] = acc[k].astype(BF16).reshape(2, n_x, 2, patches, feats)
        total = col_sum_by_core()
        terms[yb] = total.astype(BF16)
        for device, sem in ((pair, spread[0]), (outer, spread[1]), (diagonal, spread[2])):
            copy = remote(terms.at[yb], terms.at[yb], sem, device)
            copy.start()
        for wait in sent:
            wait()
        sent.clear()
        for g in range(3):
            remote(w1_in.at[g, other], w1_in.at[g, other], block_sems["outer"][g], outer).wait_recv()
            remote(w1_in.at[g, yb], w1_in.at[g, yb], block_sems["forward"][g], outer).wait_recv()
        for half_k, name in ((other, "outer"), (yb, "forward")):
            for k, (lo, hi) in ((3, (0, 2 * group)), (4, (2 * group, 3 * group))):
                part = w1_mix.at[half_k, lo:hi]
                remote(part, part, block_sems[name][k], outer).wait_recv()
        remote(gain1.at[other], gain1.at[other], block_sems["gain"][1], outer).wait_recv()
        remote(gain1.at[yb], gain1.at[yb], block_sems["gain"][2], diagonal).wait_recv()
        remote(terms.at[other], terms.at[other], spread[0], pair).wait_recv()

    x_spread = [next(sems) for _ in range(3)]
    spread = [next(sems) for _ in range(3)]
    pl.when(in_first)(first_layer)

    @pl.when(in_second)
    def _():
        remote(terms.at[other], terms.at[other], spread[1], outer).wait_recv()
        remote(terms.at[yb], terms.at[yb], spread[2], diagonal).wait_recv()
        remote(xraw.at[other], xraw.at[other], x_spread[1], outer).wait_recv()
        remote(xraw.at[yb], xraw.at[yb], x_spread[2], diagonal).wait_recv()
    for k in range(2):
        xb1[k] = (xraw[k].astype(F32) + terms[0, k].astype(F32) + terms[1, k].astype(F32)).astype(BF16)

    @pl.when(in_first)
    def _():
        y_ref[...] = xb1[yb]

    n_tok = 2 * n_col * patches
    both = xb1[...].astype(F32).reshape(2, 2 * patches, feats)
    sums = jnp.sum(jnp.sum(both, axis=-1, keepdims=True), axis=0)
    squares = jnp.sum(jnp.sum(both * both, axis=-1, keepdims=True), axis=0)
    stat1[z] = column_stats(sums, squares)
    copies = []
    for step in range(1, NZ):
        copy = remote(stat1.at[z], stat1.at[z], next(sems), {"row": yb * NZ + around(step)})
        copy.start()
        copies.append(copy)
    finish_k = []
    for k in range(2):
        gathered1[k, :, col] = xb1[k]
        finish_k.append(col_gather(lambda c, k=k: gathered1.at[k, :, c]))
    for copy in copies:
        copy.wait()
    stat_col[1, col] = lane_stats(jnp.sum(stat1[...], axis=0))
    finish_stats1 = col_direct(lambda c: stat_col.at[1, c])
    for finish in finish_k:
        finish()
    for copy in finish_stats1:
        copy.wait()
    columns1 = to_columns(stat_col[1])
    for c in range(n_col):
        for k in range(2):
            gathered1[k, :, c] = normalise(gathered1[k, :, c], columns1, c, gain1[k, 0:1])

    half_rows = 4 * patches
    short_rows = 3 * patches

    def partial_product(g):
        return (
            jnp.dot(gathered1[0].reshape(n_tok, feats), w1_in[g, 0], preferred_element_type=F32)
            + jnp.dot(gathered1[1].reshape(n_tok, feats), w1_in[g, 1], preferred_element_type=F32)
        )

    @pl.when(in_first)
    def _():
        for g in range(3):
            value = partial_product(g).reshape(NZ, 2, patches, group)
            own1[:, :, g * patches:(g + 1) * patches] = value

    @pl.when(in_second)
    def _():
        for g in range(4):
            value = partial_product(g).reshape(2, 2, half_rows, group)
            own1[g] = value[0]
            own1[4 + g] = value[1]

    def by_section(action):
        either(in_first, lambda: action(short_rows), lambda: action(half_rows))

    up1, down1 = {}, {}

    def hop1(stage, h, upward):
        send_buf, recv_buf = (zs1_p, zr1_p) if upward else (zs1_m, zr1_m)
        table = up1 if upward else down1
        device = up_z if upward else down_z
        block = around(4 - stage) if upward else around(stage - 4)
        value = own1[block, h]
        if stage >= 2 or (stage == 1 and h == (0 if upward else 1)):
            sem = table[(stage - 1, h)]
            by_section(lambda n: remote(
                recv_buf.at[stage - 1, h, 0:n], recv_buf.at[stage - 1, h, 0:n], sem, device).wait_recv())
            value = value + recv_buf[stage - 1, h].astype(F32)
        send_buf[stage, h] = value.astype(BF16)
        sem_out = next(sems)
        table[(stage, h)] = sem_out
        by_section(lambda n: remote(
            send_buf.at[stage, h, 0:n], recv_buf.at[stage, h, 0:n], sem_out, device).start())
        sent.append(lambda: by_section(lambda n: remote(
            send_buf.at[stage, h, 0:n], recv_buf.at[stage, h, 0:n], sem_out, device).wait_send()))

    hop1(0, 0, True)
    hop1(0, 1, False)
    for stage in (1, 2, 3):
        hop1(stage, 1, True)
        hop1(stage, 0, False)
        hop1(stage, 0, True)
        hop1(stage, 1, False)
    for h in (1, 0):
        by_section(lambda n: remote(zr1_p.at[3, h, 0:n], zr1_p.at[3, h, 0:n], up1[(3, h)], up_z).wait_recv())
        by_section(lambda n: remote(zr1_m.at[3, h, 0:n], zr1_m.at[3, h, 0:n], down1[(3, h)], down_z).wait_recv())

    def summed(h):
        return own1[z, h] + zr1_p[3, h].astype(F32) + zr1_m[3, h].astype(F32)

    has_head = jnp.logical_and(in_second, jnp.logical_not(wide(z)))

    @pl.when(has_head)
    def _():
        value = jnp.concatenate([summed(0), summed(1)], axis=0).astype(BF16)
        result = attend(value[:, 0:HEAD], value[:, HEAD:2 * HEAD], value[:, 2 * HEAD:3 * HEAD])
        acts1[z, :, :, 0:HEAD] = result.reshape(2, half_rows, HEAD)

    @pl.when(jnp.logical_not(has_head))
    def _():
        for h in range(2):
            acts1[z, h] = gelu(summed(h))

    def by_kind(block, action):
        either(
            in_first,
            lambda: action(short_rows, group),
            lambda: by_width(block, HEAD, group, lambda w: action(half_rows, w)),
        )

    def act_copy1(block, piece, sem, device, what):
        def action(n, w):
            part = acts1.at[block, piece // 2, (piece % 2) * (n // 2):(piece % 2 + 1) * (n // 2), 0:w]
            getattr(remote(part, part, sem, device), what)()

        by_kind(block, action)

    pieces_of_ring(act_copy1)
    @pl.when(in_first)
    def _():
        for k in range(2):
            total = None
            for g in range(3):
                hidden = acts1[:, :, g * patches:(g + 1) * patches].reshape(n_tok, group)
                term = jnp.dot(hidden, w1_mix[k, g * group:(g + 1) * group], preferred_element_type=F32)
                total = term if total is None else total + term
            acc1[k] = total

    @pl.when(in_second)
    def _():
        for image in range(2):
            first = image * 4
            value = jnp.concatenate(
                [acts1[first + j, :, :, 0:HEAD].reshape(2 * half_rows, HEAD) for j in range(3)]
                + [acts1[first + 3].reshape(2 * half_rows, group)], axis=1)
            for k in range(2):
                acc1[k, image * 2 * half_rows:(image + 1) * 2 * half_rows] = jnp.dot(
                    value, w1_mix[k, 0:2 * group], preferred_element_type=F32)

    for k in range(2):
        mix1_s[k] = acc1[k].astype(BF16).reshape(2, n_x, 2, patches, feats)
    total = col_sum()
    ys1[...] = total.astype(BF16)
    to_pair, to_outer, to_diagonal = next(sems), next(sems), next(sems)

    @pl.when(in_first)
    def _():
        copies = [remote(ys1.at[other], yr1.at[1], to_outer, outer), remote(ys1.at[yb], yr1.at[2], to_diagonal, diagonal)]
        for copy in copies:
            copy.start()
        for copy in copies:
            copy.wait_send()

    @pl.when(in_second)
    def _():
        copy = remote(ys1.at[other], yr1.at[0], to_pair, pair)
        copy.start()
        copy.wait()
        remote(yr1.at[1], yr1.at[1], to_outer, outer).wait_recv()
        remote(yr1.at[2], yr1.at[2], to_diagonal, diagonal).wait_recv()
        result = xb1[yb].astype(F32) + ys1[yb].astype(F32)
        for k in range(3):
            result = result + yr1[k].astype(F32)
        y_ref[...] = result.astype(BF16)

    assert next(sems) < 288
    for wait in sent:
        wait()

    @pl.when(in_first)
    def _():
        for device, sem in ((pair, spread[0]), (outer, spread[1]), (diagonal, spread[2])):
            remote(terms.at[yb], terms.at[yb], sem, device).wait_send()


def layers(x, weights):
    gain, wq, wk, wv, wup, wout, wdown = weights
    n_col = lax.axis_size("col")
    images, patches, feats = x.shape
    wide_in = 6 * HEAD
    vmem = pl.BlockSpec(memory_space=pltpu.VMEM)
    anywhere = pl.BlockSpec(memory_space=pl.ANY)
    rows = n_col * patches
    late = rows // 2
    early = rows - late
    g_buf = pltpu.VMEM((4, 2, rows // 2, 2 * HEAD), BF16)
    z_buf = pltpu.VMEM((4, 2, late, 4 * HEAD), BF16)
    y_buf = pltpu.VMEM((4, 2, early // 2, 4 * HEAD), BF16)
    pair_buf = pltpu.VMEM((NZ, early, 4 * HEAD), BF16)
    z1_buf = pltpu.VMEM((4, 2, 4 * patches, feats), BF16)
    scratch = [
        pltpu.VMEM((NZ, feats, wide_in), BF16),
        pltpu.VMEM((NZ, wide_in, feats), BF16),
        pltpu.VMEM((NZ, feats, 4 * HEAD), BF16),
        pltpu.VMEM((4, 2, feats, 2 * HEAD), BF16),
        pltpu.VMEM((4, feats, 2 * HEAD), BF16),
        pltpu.VMEM((4, wide_in, feats), BF16),
        pltpu.VMEM((2, 2, n_col, patches, feats), BF16),
        pltpu.VMEM((2, 8, feats), F32),
        pltpu.VMEM((NZ, 2, rows, 4 * HEAD), F32),
        pltpu.VMEM((4, 2, 2, rows // 2, 2 * HEAD), F32),
        pltpu.VMEM((2 * NZ, 8, 128), F32),
        g_buf, g_buf, g_buf, g_buf, z_buf, z_buf, z_buf, z_buf, y_buf, y_buf, y_buf, y_buf, pair_buf, pair_buf,
        pltpu.VMEM((late, 4 * HEAD), BF16), pltpu.VMEM((late, 4 * HEAD), BF16),
        pltpu.VMEM((rows, 4 * HEAD), F32),
        pltpu.VMEM((NZ, 2, rows // 2, wide_in), BF16),
        pltpu.VMEM((2, 2, rows, feats), F32),
        pltpu.VMEM((2, n_col, 8, 128), F32),
        pltpu.VMEM((2, 2, patches, feats), BF16),
        pltpu.VMEM((2, 2, 2, patches, feats), BF16),
        pltpu.VMEM((2, 2, n_col // 2, patches, feats), BF16),
        pltpu.VMEM((2, 2, n_col // 2, patches, feats), BF16),
        pltpu.VMEM((n_col // 2 - 1, 2, 2, patches, feats), BF16),
        pltpu.VMEM((4, 2, feats, feats), BF16),
        pltpu.VMEM((2, 3 * feats, feats), BF16),
        pltpu.VMEM((2, 8, feats), F32),
        pltpu.VMEM((2, 2, patches, feats), BF16),
        pltpu.VMEM((2, 2, n_col, patches, feats), BF16),
        pltpu.VMEM((NZ, 2, 4 * patches, feats), F32),
        pltpu.VMEM((NZ, 8, 128), F32),
        z1_buf, z1_buf, z1_buf, z1_buf,
        pltpu.VMEM((NZ, 2, 4 * patches, feats), BF16),
        pltpu.VMEM((2, 2 * n_col * patches, feats), F32),
        pltpu.VMEM((2, 2, n_col // 2, 2, patches, feats), BF16),
        pltpu.VMEM((n_col - 1, 2, 2, patches, feats), BF16),
        pltpu.VMEM((2, 2, patches, feats), BF16),
        pltpu.VMEM((3, 2, patches, feats), BF16),
        pltpu.SemaphoreType.DMA((64,)),
        pltpu.SemaphoreType.DMA((288,)),
        pltpu.SemaphoreType.DMA((288,)),
    ]
    return pl.pallas_call(
        functools.partial(layers_kernel, n_col, patches, feats),
        out_shape=jax.ShapeDtypeStruct(x.shape, BF16),
        in_specs=[vmem, vmem] + [anywhere] * 6,
        out_specs=vmem,
        scratch_shapes=scratch,
        compiler_params=pltpu.CompilerParams(
            collective_id=0, has_side_effects=True, vmem_limit_bytes=67043328
        ),
    )(x, gain[None], wq, wk, wv, wup, wout, wdown)


def local(tokens, ln_gain, w_query, w_key, w_value, w_up, w_out, w_down):
    weights = (ln_gain[0], w_query[0], w_key[0], w_value[0], w_up[0], w_out[0], w_down[0])
    return layers(tokens, weights)[None]


def solution(mesh):
    return jax.shard_map(
        local,
        mesh=mesh,
        in_specs=(
            P(None, "col", "row"),
            P("section", "row"),
            P("section", "row", "col"),
            P("section", "row", "col"),
            P("section", "row", "col"),
            P("section", "row", "col"),
            P("section", "col", "row"),
            P("section", "col", "row"),
        ),
        out_specs=P("section", None, "col", "row"),
        check_vma=False,
    )
```

time: 174 us -> 162 us (0.931); the launches traced: 171 us -> 162 us
  Pallas kernels: 170 us -> 161 us
    pallas_call x1, Pallas kernels: 170 us -> 161 us  [layers(): pl.pallas_call(functools.partial(layers_kernel, n_col, patches, feats), o...]
where the time goes in v4:
time: 162 us
  Pallas kernels  161 us (99%)
    pallas_call x1, Pallas kernels, layers(): pl.pallas_call(functools.partial(layers_kernel, n_col, patches, feats), o...  161 us

profile of v4, /device:TPU:17, one launch (start us, length us, event | category | flops | bytes accessed | tf_op | source)
XLA Modules:
  0.0 162.0 jit_solution(17147636583138720522)
XLA Ops:
  0.0 160.6 %shard_map.82 = bf16[2,32,384]{2,1,0:T(8,128)(2,1)} custom-call(bf16[2,32,384]{2,1,0:T(8,128)(2,1)} %x_ref.1, f32[1,384]{1,0:T(1,128)} %gain_ref.1, bf16[384,768]{1,0:T(8,128)(2,1)} %bitcast.9, bf16[384,768]{1,0:T(8,128)(2,1)} %bitcast.10, bf16[384,768]{1,0:T(8,128)(2,1)} %bitcast.11, bf16[384,3072]{1,0:T(8,128)(2,1)} %bitcast.7, bf16[768,384]{1,0:T(8,128)(2,1)} %bitcast.12, ...), custom_call_target="tpu_custom_call" | custom-call | tf_op jit(solution)/shard_map/pallas_call | solution.py:949
  160.6 1.4 copy.10

commit v5 on v4

--- a/solution.py
+++ b/solution.py
@@ -179,17 +179,22 @@
         return value
 
     def col_sum_by_core():
-        swap = remote(mix1_s.at[:, :, :, 1 - core], mix_d, next(sems), sibling)
-        swap.start()
-        swap.wait()
+        swaps = []
+        for step in (2, 1, 3, 0):
+            target = along_x(step)
+            swap = remote(mix1_s.at[:, :, target, 1 - core], mix_d.at[:, :, target], next(sems), sibling)
+            swap.start()
+            swaps.append(swap)
         copies = []
-        for step in (2, 1, 3):
+        for step, swap in zip((2, 1, 3), swaps):
             target = along_x(step)
+            swap.wait()
             mix_t[:, :, target] = (
                 mix1_s[:, :, target, core].astype(F32) + mix_d[:, :, target].astype(F32)).astype(BF16)
             copy = remote(mix_t.at[:, :, target], mix_e.at[step - 1], next(sems), same_core(step))
             copy.start()
             copies.append((copy, step - 1))
+        swaps[3].wait()
         value = mix1_s[:, :, chip_x, core].astype(F32) + mix_d[:, :, chip_x].astype(F32)
         for copy, slot in copies:
             copy.wait()
@@ -345,6 +350,38 @@
 
         for g in range(4):
             fetch(wup_ref.at[:, columns_at(member_hidden(other, g)[1], part_g)], w_gs.at[g], "stage")
+        xf = x_ref[...].astype(F32).reshape(2 * patches, feats)
+        sums = jnp.sum(xf, axis=-1, keepdims=True)
+        squares = jnp.sum(xf * xf, axis=-1, keepdims=True)
+        stat[row] = column_stats(sums, squares)
+        xraw[yb] = x_ref[...]
+        gathered[yb, :, col] = x_ref[...]
+        gain0[yb] = jnp.broadcast_to(gain_ref[...], (8, feats))
+        ready()
+        x_copy = remote(xraw.at[yb], xraw.at[yb], x_spread[0], pair)
+        x_copy.start()
+        stat_copies = []
+        for step in range(1, n_row):
+            copy = remote(stat.at[row], stat.at[row], next(sems), {"row": lax.rem(row + step, n_row)})
+            copy.start()
+            stat_copies.append(copy)
+        finish_own = col_gather(lambda c: gathered.at[yb, :, c])
+        gain_copy = remote(gain0.at[yb], gain0.at[yb], next(sems), pair)
+        gain_copy.start()
+        for device, sem in ((outer, x_spread[1]), (diagonal, x_spread[2])):
+            copy = remote(xraw.at[yb], xraw.at[yb], sem, device)
+            copy.start()
+            sent.append(copy.wait_send)
+
+        def group_at(i):
+            return lax.rem(z + (0, 3, 1, 2)[i], 4)
+
+        def traced_group_at(i):
+            return lax.rem(z + jnp.where(i == 0, 0, jnp.where(i == 1, 3, i - 1)), 4)
+
+        g_base = next(sems)
+        for _ in range(3):
+            next(sems)
         for g in range(4):
             fetch(wup_ref.at[:, columns_at(member_hidden(yb, g)[1], part_g)], w_g.at[g, yb], "own")
         for block in range(NZ):
@@ -365,39 +402,6 @@
                 else:
                     fetch(wout_ref.at[columns_at((member * 3 + g) * HEAD, HEAD)], target.at[0:HEAD], kind)
                     fetch(wdn_ref.at[rows], target.at[HEAD:narrow_mix], kind)
-
-        xf = x_ref[...].astype(F32).reshape(2 * patches, feats)
-        sums = jnp.sum(xf, axis=-1, keepdims=True)
-        squares = jnp.sum(xf * xf, axis=-1, keepdims=True)
-        stat[row] = column_stats(sums, squares)
-        xraw[yb] = x_ref[...]
-        gathered[yb, :, col] = x_ref[...]
-        gain0[yb] = jnp.broadcast_to(gain_ref[...], (8, feats))
-        ready()
-        x_copy = remote(xraw.at[yb], xraw.at[yb], x_spread[0], pair)
-        x_copy.start()
-        stat_copies = []
-        for step in range(1, n_row):
-            copy = remote(stat.at[row], stat.at[row], next(sems), {"row": lax.rem(row + step, n_row)})
-            copy.start()
-            stat_copies.append(copy)
-        finish_own = col_gather(lambda c: gathered.at[yb, :, c])
-        gain_copy = remote(gain0.at[yb], gain0.at[yb], next(sems), pair)
-        gain_copy.start()
-        for device, sem in ((outer, x_spread[1]), (diagonal, x_spread[2])):
-            copy = remote(xraw.at[yb], xraw.at[yb], sem, device)
-            copy.start()
-            sent.append(copy.wait_send)
-
-        def group_at(i):
-            return lax.rem(z + (0, 3, 1, 2)[i], 4)
-
-        def traced_group_at(i):
-            return lax.rem(z + jnp.where(i == 0, 0, jnp.where(i == 1, 3, i - 1)), 4)
-
-        g_base = next(sems)
-        for _ in range(3):
-            next(sems)
         for copy in waits["stage"]:
             copy.wait()
         for i in range(4):
@@ -745,8 +749,9 @@
         for k in range(2):
             gathered1[k, :, c] = normalise(gathered1[k, :, c], columns1, c, gain1[k, 0:1])
 
-    half_rows = 4 * patches
-    short_rows = 3 * patches
+    piece_long = 2 * patches
+    piece_short = 3 * patches // 2
+    third_rows = patches // 2
 
     def partial_product(g):
         return (
@@ -757,20 +762,23 @@
     @pl.when(in_first)
     def _():
         for g in range(3):
-            value = partial_product(g).reshape(NZ, 2, patches, group)
-            own1[:, :, g * patches:(g + 1) * patches] = value
+            value = partial_product(g).reshape(NZ, 4, third_rows, group)
+            own1[:, :, g * third_rows:(g + 1) * third_rows] = value
 
     @pl.when(in_second)
     def _():
         for g in range(4):
-            value = partial_product(g).reshape(2, 2, half_rows, group)
+            value = partial_product(g).reshape(2, 4, piece_long, group)
             own1[g] = value[0]
             own1[4 + g] = value[1]
 
     def by_section(action):
-        either(in_first, lambda: action(short_rows), lambda: action(half_rows))
+        either(in_first, lambda: action(piece_short), lambda: action(piece_long))
 
     up1, down1 = {}, {}
+
+    def far(h, upward):
+        return (h < 2) == upward
 
     def hop1(stage, h, upward):
         send_buf, recv_buf = (zs1_p, zr1_p) if upward else (zs1_m, zr1_m)
@@ -778,7 +786,7 @@
         device = up_z if upward else down_z
         block = around(4 - stage) if upward else around(stage - 4)
         value = own1[block, h]
-        if stage >= 2 or (stage == 1 and h == (0 if upward else 1)):
+        if stage >= 2 or (stage == 1 and far(h, upward)):
             sem = table[(stage - 1, h)]
             by_section(lambda n: remote(
                 recv_buf.at[stage - 1, h, 0:n], recv_buf.at[stage - 1, h, 0:n], sem, device).wait_recv())
@@ -791,14 +799,14 @@
         sent.append(lambda: by_section(lambda n: remote(
             send_buf.at[stage, h, 0:n], recv_buf.at[stage, h, 0:n], sem_out, device).wait_send()))
 
-    hop1(0, 0, True)
-    hop1(0, 1, False)
+    for h in (0, 1):
+        hop1(0, h, True)
+        hop1(0, h + 2, False)
     for stage in (1, 2, 3):
-        hop1(stage, 1, True)
-        hop1(stage, 0, False)
-        hop1(stage, 0, True)
-        hop1(stage, 1, False)
-    for h in (1, 0):
+        for h in (2, 3, 0, 1):
+            hop1(stage, h, True)
+            hop1(stage, (h + 2) % 4, False)
+    for h in range(4):
         by_section(lambda n: remote(zr1_p.at[3, h, 0:n], zr1_p.at[3, h, 0:n], up1[(3, h)], up_z).wait_recv())
         by_section(lambda n: remote(zr1_m.at[3, h, 0:n], zr1_m.at[3, h, 0:n], down1[(3, h)], down_z).wait_recv())
 
@@ -809,25 +817,25 @@
 
     @pl.when(has_head)
     def _():
-        value = jnp.concatenate([summed(0), summed(1)], axis=0).astype(BF16)
+        value = jnp.concatenate([summed(h) for h in range(4)], axis=0).astype(BF16)
         result = attend(value[:, 0:HEAD], value[:, HEAD:2 * HEAD], value[:, 2 * HEAD:3 * HEAD])
-        acts1[z, :, :, 0:HEAD] = result.reshape(2, half_rows, HEAD)
+        acts1[z, :, :, 0:HEAD] = result.reshape(4, piece_long, HEAD)
 
     @pl.when(jnp.logical_not(has_head))
     def _():
-        for h in range(2):
+        for h in range(4):
             acts1[z, h] = gelu(summed(h))
 
     def by_kind(block, action):
         either(
             in_first,
-            lambda: action(short_rows, group),
-            lambda: by_width(block, HEAD, group, lambda w: action(half_rows, w)),
+            lambda: action(piece_short, group),
+            lambda: by_width(block, HEAD, group, lambda w: action(piece_long, w)),
         )
 
     def act_copy1(block, piece, sem, device, what):
         def action(n, w):
-            part = acts1.at[block, piece // 2, (piece % 2) * (n // 2):(piece % 2 + 1) * (n // 2), 0:w]
+            part = acts1.at[block, piece, 0:n, 0:w]
             getattr(remote(part, part, sem, device), what)()
 
         by_kind(block, action)
@@ -838,7 +846,7 @@
         for k in range(2):
             total = None
             for g in range(3):
-                hidden = acts1[:, :, g * patches:(g + 1) * patches].reshape(n_tok, group)
+                hidden = acts1[:, :, g * third_rows:(g + 1) * third_rows].reshape(n_tok, group)
                 term = jnp.dot(hidden, w1_mix[k, g * group:(g + 1) * group], preferred_element_type=F32)
                 total = term if total is None else total + term
             acc1[k] = total
@@ -848,10 +856,10 @@
         for image in range(2):
             first = image * 4
             value = jnp.concatenate(
-                [acts1[first + j, :, :, 0:HEAD].reshape(2 * half_rows, HEAD) for j in range(3)]
-                + [acts1[first + 3].reshape(2 * half_rows, group)], axis=1)
+                [acts1[first + j, :, :, 0:HEAD].reshape(image_rows, HEAD) for j in range(3)]
+                + [acts1[first + 3].reshape(image_rows, group)], axis=1)
             for k in range(2):
-                acc1[k, image * 2 * half_rows:(image + 1) * 2 * half_rows] = jnp.dot(
+                acc1[k, image * image_rows:(image + 1) * image_rows] = jnp.dot(
                     value, w1_mix[k, 0:2 * group], preferred_element_type=F32)
 
     for k in range(2):
@@ -880,7 +888,7 @@
             result = result + yr1[k].astype(F32)
         y_ref[...] = result.astype(BF16)
 
-    assert next(sems) < 288
+    assert next(sems) < 304
     for wait in sent:
         wait()
 
@@ -904,7 +912,7 @@
     z_buf = pltpu.VMEM((4, 2, late, 4 * HEAD), BF16)
     y_buf = pltpu.VMEM((4, 2, early // 2, 4 * HEAD), BF16)
     pair_buf = pltpu.VMEM((NZ, early, 4 * HEAD), BF16)
-    z1_buf = pltpu.VMEM((4, 2, 4 * patches, feats), BF16)
+    z1_buf = pltpu.VMEM((4, 4, 2 * patches, feats), BF16)
     scratch = [
         pltpu.VMEM((NZ, feats, wide_in), BF16),
         pltpu.VMEM((NZ, wide_in, feats), BF16),
@@ -933,18 +941,18 @@
         pltpu.VMEM((2, 8, feats), F32),
         pltpu.VMEM((2, 2, patches, feats), BF16),
         pltpu.VMEM((2, 2, n_col, patches, feats), BF16),
-        pltpu.VMEM((NZ, 2, 4 * patches, feats), F32),
+        pltpu.VMEM((NZ, 4, 2 * patches, feats), F32),
         pltpu.VMEM((NZ, 8, 128), F32),
         z1_buf, z1_buf, z1_buf, z1_buf,
-        pltpu.VMEM((NZ, 2, 4 * patches, feats), BF16),
+        pltpu.VMEM((NZ, 4, 2 * patches, feats), BF16),
         pltpu.VMEM((2, 2 * n_col * patches, feats), F32),
         pltpu.VMEM((2, 2, n_col // 2, 2, patches, feats), BF16),
         pltpu.VMEM((n_col - 1, 2, 2, patches, feats), BF16),
         pltpu.VMEM((2, 2, patches, feats), BF16),
         pltpu.VMEM((3, 2, patches, feats), BF16),
         pltpu.SemaphoreType.DMA((64,)),
-        pltpu.SemaphoreType.DMA((288,)),
-        pltpu.SemaphoreType.DMA((288,)),
+        pltpu.SemaphoreType.DMA((304,)),
+        pltpu.SemaphoreType.DMA((304,)),
     ]
     return pl.pallas_call(
         functools.partial(layers_kernel, n_col, patches, feats),

time: 162 us -> 162 us (level)
  no operation moved by 1% of the time
where the time goes in v5:
time: 162 us
  Pallas kernels  160 us (99%)
    pallas_call x1, Pallas kernels, layers(): pl.pallas_call(functools.partial(layers_kernel, n_col, patches, feats), o...  160 us

profile of v5, /device:TPU:17, one launch (start us, length us, event | category | flops | bytes accessed | tf_op | source)
XLA Modules:
  0.0 161.7 jit_solution(16659870487526981294)
XLA Ops:
  0.0 160.3 %shard_map.82 = bf16[2,32,384]{2,1,0:T(8,128)(2,1)} custom-call(bf16[2,32,384]{2,1,0:T(8,128)(2,1)} %x_ref.1, f32[1,384]{1,0:T(1,128)} %gain_ref.1, bf16[384,768]{1,0:T(8,128)(2,1)} %bitcast.9, bf16[384,768]{1,0:T(8,128)(2,1)} %bitcast.10, bf16[384,768]{1,0:T(8,128)(2,1)} %bitcast.11, bf16[384,3072]{1,0:T(8,128)(2,1)} %bitcast.7, bf16[768,384]{1,0:T(8,128)(2,1)} %bitcast.12, ...), custom_call_target="tpu_custom_call" | custom-call | tf_op jit(solution)/shard_map/pallas_call | solution.py:957
  160.3 1.4 copy.10

commit v6 on v5

--- a/solution.py
+++ b/solution.py
@@ -165,18 +165,6 @@
             copy.start()
             copies.append(copy)
         return copies
-
-    def col_sum():
-        copies = []
-        for slot, target_x, target_core, device in col_peers():
-            copy = remote(mix1_s.at[:, :, target_x, target_core], mix_r.at[slot], next(sems), device)
-            copy.start()
-            copies.append((copy, slot))
-        value = mix1_s[:, :, chip_x, core].astype(F32)
-        for copy, slot in copies:
-            copy.wait()
-            value = value + mix_r[slot].astype(F32)
-        return value
 
     def col_sum_by_core():
         swaps = []
@@ -840,31 +828,51 @@
 
         by_kind(block, action)
 
-    pieces_of_ring(act_copy1)
-    @pl.when(in_first)
-    def _():
-        for k in range(2):
-            total = None
-            for g in range(3):
-                hidden = acts1[:, :, g * third_rows:(g + 1) * third_rows].reshape(n_tok, group)
-                term = jnp.dot(hidden, w1_mix[k, g * group:(g + 1) * group], preferred_element_type=F32)
-                total = term if total is None else total + term
-            acc1[k] = total
-
-    @pl.when(in_second)
-    def _():
-        for image in range(2):
-            first = image * 4
+    image_sums = []
+
+    def send_image(image):
+        first = image * 4
+        span = pl.ds(pl.multiple_of(image * image_rows, image_rows), image_rows)
+
+        @pl.when(in_first)
+        def _():
+            for k in range(2):
+                total = None
+                for g in range(3):
+                    hidden = acts1[pl.ds(first, 4), :, g * third_rows:(g + 1) * third_rows].reshape(image_rows, group)
+                    term = jnp.dot(hidden, w1_mix[k, g * group:(g + 1) * group], preferred_element_type=F32)
+                    total = term if total is None else total + term
+                acc1[k, span] = total
+
+        @pl.when(in_second)
+        def _():
             value = jnp.concatenate(
                 [acts1[first + j, :, :, 0:HEAD].reshape(image_rows, HEAD) for j in range(3)]
                 + [acts1[first + 3].reshape(image_rows, group)], axis=1)
             for k in range(2):
-                acc1[k, image * image_rows:(image + 1) * image_rows] = jnp.dot(
-                    value, w1_mix[k, 0:2 * group], preferred_element_type=F32)
-
-    for k in range(2):
-        mix1_s[k] = acc1[k].astype(BF16).reshape(2, n_x, 2, patches, feats)
-    total = col_sum()
+                acc1[k, span] = jnp.dot(value, w1_mix[k, 0:2 * group], preferred_element_type=F32)
+
+        for k in range(2):
+            mix1_s[k, image] = acc1[k, span].astype(BF16).reshape(n_x, 2, patches, feats)
+        for slot, target_x, target_core, device in col_peers():
+            copy = remote(
+                mix1_s.at[:, image, target_x, target_core], mix_r.at[slot, :, image], next(sems), device)
+            copy.start()
+            image_sums.append(copy)
+
+    near = lax.div(z, 4)
+
+    def after_stage1(stage):
+        if stage == 2:
+            send_image(near)
+
+    pieces_of_ring(act_copy1, after_stage1)
+    send_image(1 - near)
+    for copy in image_sums:
+        copy.wait()
+    total = mix1_s[:, :, chip_x, core].astype(F32)
+    for slot in range(n_col - 1):
+        total = total + mix_r[slot].astype(F32)
     ys1[...] = total.astype(BF16)
     to_pair, to_outer, to_diagonal = next(sems), next(sems), next(sems)
 
@@ -888,7 +896,7 @@
             result = result + yr1[k].astype(F32)
         y_ref[...] = result.astype(BF16)
 
-    assert next(sems) < 304
+    assert next(sems) < 320
     for wait in sent:
         wait()
 
@@ -951,8 +959,8 @@
         pltpu.VMEM((2, 2, patches, feats), BF16),
         pltpu.VMEM((3, 2, patches, feats), BF16),
         pltpu.SemaphoreType.DMA((64,)),
-        pltpu.SemaphoreType.DMA((304,)),
-        pltpu.SemaphoreType.DMA((304,)),
+        pltpu.SemaphoreType.DMA((320,)),
+        pltpu.SemaphoreType.DMA((320,)),
     ]
     return pl.pallas_call(
         functools.partial(layers_kernel, n_col, patches, feats),

time: 162 us -> 160 us (0.988)
  no operation moved by 1% of the time
where the time goes in v6:
time: 160 us
  Pallas kernels  159 us (99%)
    pallas_call x1, Pallas kernels, layers(): pl.pallas_call(functools.partial(layers_kernel, n_col, patches, feats), o...  159 us

profile of v6, /device:TPU:17, one launch (start us, length us, event | category | flops | bytes accessed | tf_op | source)
XLA Modules:
  0.0 160.2 jit_solution(15010636365502783376)
XLA Ops:
  0.0 158.7 %shard_map.82 = bf16[2,32,384]{2,1,0:T(8,128)(2,1)} custom-call(bf16[2,32,384]{2,1,0:T(8,128)(2,1)} %x_ref.1, f32[1,384]{1,0:T(1,128)} %gain_ref.1, bf16[384,768]{1,0:T(8,128)(2,1)} %bitcast.9, bf16[384,768]{1,0:T(8,128)(2,1)} %bitcast.10, bf16[384,768]{1,0:T(8,128)(2,1)} %bitcast.11, bf16[384,3072]{1,0:T(8,128)(2,1)} %bitcast.7, bf16[768,384]{1,0:T(8,128)(2,1)} %bitcast.12, ...), custom_call_target="tpu_custom_call" | custom-call | tf_op jit(solution)/shard_map/pallas_call | solution.py:965
  158.7 1.4 copy.10

commit v7 on v6

--- a/solution.py
+++ b/solution.py
@@ -356,10 +356,6 @@
         finish_own = col_gather(lambda c: gathered.at[yb, :, c])
         gain_copy = remote(gain0.at[yb], gain0.at[yb], next(sems), pair)
         gain_copy.start()
-        for device, sem in ((outer, x_spread[1]), (diagonal, x_spread[2])):
-            copy = remote(xraw.at[yb], xraw.at[yb], sem, device)
-            copy.start()
-            sent.append(copy.wait_send)
 
         def group_at(i):
             return lax.rem(z + (0, 3, 1, 2)[i], 4)
@@ -588,6 +584,10 @@
         sent.append(lambda: move("Z", last_s, last_s, last_sem, pair, z, "wait_send"))
         for g in (3, 0, 1, 2):
             send_mix(g)
+        for device, sem in ((outer, x_spread[1]), (diagonal, x_spread[2])):
+            copy = remote(xraw.at[yb], xraw.at[yb], sem, device)
+            copy.start()
+            sent.append(copy.wait_send)
         four("Y", 1, (1, 2))
         four("G", 3)
         four("Y", 2, (3, 4))

time: 160 us -> 160 us (level)
  no operation moved by 1% of the time
where the time goes in v7:
time: 160 us
  Pallas kernels  158 us (99%)
    pallas_call x1, Pallas kernels, layers(): pl.pallas_call(functools.partial(layers_kernel, n_col, patches, feats), o...  158 us

profile of v7, /device:TPU:17, one launch (start us, length us, event | category | flops | bytes accessed | tf_op | source)
XLA Modules:
  0.0 159.7 jit_solution(4748832096133446309)
XLA Ops:
  0.0 158.2 %shard_map.82 = bf16[2,32,384]{2,1,0:T(8,128)(2,1)} custom-call(bf16[2,32,384]{2,1,0:T(8,128)(2,1)} %x_ref.1, f32[1,384]{1,0:T(1,128)} %gain_ref.1, bf16[384,768]{1,0:T(8,128)(2,1)} %bitcast.9, bf16[384,768]{1,0:T(8,128)(2,1)} %bitcast.10, bf16[384,768]{1,0:T(8,128)(2,1)} %bitcast.11, bf16[384,3072]{1,0:T(8,128)(2,1)} %bitcast.7, bf16[768,384]{1,0:T(8,128)(2,1)} %bitcast.12, ...), custom_call_target="tpu_custom_call" | custom-call | tf_op jit(solution)/shard_map/pallas_call | solution.py:965
  158.2 1.4 copy.10
